TPU v7x, 128 devices: a whole 4x4x4 slice. The times are simulated.
128 devices in a mesh: parts: 1, data: 128 (over z, y, x, core).
Axes of the slice: x: 4, y: 4, z: 4, core: 2. Of those that a mesh axis runs over, the one named last changes fastest.
Arguments:
- feats: bfloat16 [131072, 123], P('data')
- labels: int32 [131072], P('data')
- w_in: float32 [123, 64, 50], P(None, 'parts')
- w_out: float32 [64, 50], P('parts')
- mom_in: float32 [123, 64, 50], P(None, 'parts')
- mom_out: float32 [64, 50], P('parts')
Outputs:
- output 1: float32 [123, 64, 50], P(None, 'parts')
- output 2: float32 [64, 50], P('parts')
- output 3: float32 [123, 64, 50], P(None, 'parts')
- output 4: float32 [64, 50], P('parts')
- output 5: float32 [64], P('parts')
All inputs are finite; a program needn't handle non-finite values.
Results may differ from a plain program's by a relative error of at most 0.001.
Values are sent between devices in bfloat16 or wider.
A program may use at most 1 GiB of HBM per device.

v0:
```python
import math
import jax
import jax.numpy as jnp
from jax import lax
from jax.sharding import PartitionSpec as P

LEAPS = 16
PRIOR_VAR = 1.0


def local_terms(x_rows, lab_rows, w_flat, pos_out):
    num_chain, hidden = pos_out.shape
    num_rows = x_rows.shape[0]
    pre_act = jnp.dot(x_rows, w_flat, preferred_element_type=jnp.float32).reshape(num_rows, num_chain, hidden)
    hidden_act = jnp.tanh(pre_act)
    logits = jnp.sum(hidden_act * pos_out, axis=-1)
    residual = lab_rows[:, None] - jax.nn.sigmoid(logits)
    grad_out = jnp.sum(hidden_act * residual[:, :, None], axis=0)
    back_grad = (residual[:, :, None] * pos_out * (1.0 - hidden_act * hidden_act)).astype(jnp.bfloat16)
    grad_in = lax.dot_general(x_rows, back_grad.reshape(num_rows, num_chain * hidden), (((0,), (0,)), ((), ())), preferred_element_type=jnp.float32)
    return grad_in.reshape(w_flat.shape[0], num_chain, hidden), grad_out, logits


def solution(mesh):
    row_spec = P('data', None)
    label_spec = P('data')
    in_spec = P(None, 'parts', None)
    out_spec = P('parts', None)
    chain_spec = P('parts')

    def run_chains(feats, labels, w_in, w_out, mom_in, mom_out):
        num_rows, num_feat = feats.shape
        hidden = w_in.shape[2]
        step_size = 1.0 / math.sqrt(num_rows * (num_feat + hidden))
        half_step = 0.5 * step_size

        def device_body(x_rows, y_rows, pos_in, pos_out, vel_in, vel_out):
            lab_rows = y_rows.astype(jnp.float32)
            num_chain = pos_out.shape[0]

            def log_post_grad(pos_in, pos_out):
                w_flat = pos_in.astype(jnp.bfloat16).reshape(num_feat, num_chain * hidden)
                grad_in, grad_out, logits = local_terms(x_rows, lab_rows, w_flat, pos_out)
                grad_in, grad_out = lax.psum((grad_in, grad_out), 'data')
                return grad_in - pos_in / PRIOR_VAR, grad_out - pos_out / PRIOR_VAR, logits

            def leap_step(step_index, state_now):
                pos_in, pos_out, vel_in, vel_out = state_now
                pos_in = pos_in + step_size * vel_in
                pos_out = pos_out + step_size * vel_out
                grad_in, grad_out, logits = log_post_grad(pos_in, pos_out)
                return pos_in, pos_out, vel_in + step_size * grad_in, vel_out + step_size * grad_out

            grad_in, grad_out, logits = log_post_grad(pos_in, pos_out)
            vel_in = vel_in + half_step * grad_in
            vel_out = vel_out + half_step * grad_out
            pos_in, pos_out, vel_in, vel_out = lax.fori_loop(0, LEAPS - 1, leap_step, (pos_in, pos_out, vel_in, vel_out))
            pos_in = pos_in + step_size * vel_in
            pos_out = pos_out + step_size * vel_out
            grad_in, grad_out, logits = log_post_grad(pos_in, pos_out)
            vel_in = vel_in + half_step * grad_in
            vel_out = vel_out + half_step * grad_out
            row_loss = jnp.sum(jax.nn.softplus(logits) - lab_rows[:, None] * logits, axis=0)
            row_loss = lax.psum(row_loss, 'data')
            energy = row_loss + (jnp.sum(pos_in * pos_in, axis=(0, 2)) + jnp.sum(pos_out * pos_out, axis=1)) / (2.0 * PRIOR_VAR) + 0.5 * (jnp.sum(vel_in * vel_in, axis=(0, 2)) + jnp.sum(vel_out * vel_out, axis=1))
            return pos_in, pos_out, vel_in, vel_out, energy

        mapped = jax.shard_map(device_body, mesh=mesh, in_specs=(row_spec, label_spec, in_spec, out_spec, in_spec, out_spec), out_specs=(in_spec, out_spec, in_spec, out_spec, chain_spec), check_vma=False)
        return mapped(feats, labels, w_in, w_out, mom_in, mom_out)

    return run_chains
```

profile of v0, /device:TPU:1, one launch (start us, length us, event | category | flops | bytes accessed | tf_op | source)
XLA Modules:
  0.0 3684.9 jit_solution(5399495571537027620)
XLA Ops:
  40.5 69.5 %psum.50 = f32[64,50]{0,1:T(8,128)S(1)} all-reduce(f32[64,50]{0,1:T(8,128)S(1)} %get-tuple-element.106), channel_id=1, replica_groups=mesh['parts'=1,'data'=128] {'data'}, use_global_device_ids=true, to_apply=%region_3.0 | all-reduce | flops 3200 | bytes 25600 | tf_op jit(solution)/shard_map/psum | solution.py:44
  110.1 85.5 %all-reduce.5.cloned.1.call-done = f32[123,64,50]{0,2,1:T(8,128)} async-done(((f32[123,64,50]{0,2,1:T(8,128)}), f32[123,64,50]{0,2,1:T(8,128)}) %all-reduce.5.cloned.1.call-update) | async-done | bytes 1574416 | tf_op jit(solution)/shard_map/psum | solution.py:44
  201.5 3244.9 %while.16 = (s32[]{:T(128)}, f32[123,64,50]{0,2,1:T(8,128)}, f32[64,50]{1,0:T(8,128)S(1)}, f32[123,64,50]{0,2,1:T(8,128)S(1)}, f32[64,50]{1,0:T(8,128)S(1)}, /*i...) while((s32[]{:T(128)}, f32[123,64,50]{0,2,1:T(8,128)}, ...), condition=%wide.region_9.0_spmd, body=%wide.region_4.0_spmd.sunk | while | flops 1644644608 | bytes 175808656 | solution.py:57
  273.7 64.9 %psum.57 = f32[64,50]{1,0:T(8,128)S(1)} all-reduce(f32[64,50]{1,0:T(8,128)S(1)} %reduce_sum.129), channel_id=1, replica_groups=mesh['parts'=1,'data'=128] {'data'}, use_global_device_ids=true, to_apply=%region_8.0 | all-reduce | flops 3200 | bytes 25600 | tf_op jit(solution)/shard_map/while/body/eval_jaxpr/psum | solution.py:44
  338.6 75.9 %all-reduce.9.cloned.1.call-done = f32[123,64,50]{0,2,1:T(8,128)} async-done(((f32[123,64,50]{0,2,1:T(8,128)}), f32[123,64,50]{0,2,1:T(8,128)}) %all-reduce.9.cloned.1.call-update) | async-done | bytes 1574416 | tf_op jit(solution)/shard_map/while/body/eval_jaxpr/psum | solution.py:44
  554.9 75.9 %all-reduce.9.cloned.1.call-done = f32[123,64,50]{0,2,1:T(8,128)} async-done(((f32[123,64,50]{0,2,1:T(8,128)}), f32[123,64,50]{0,2,1:T(8,128)}) %all-reduce.9.cloned.1.call-update) | async-done | bytes 1574416 | tf_op jit(solution)/shard_map/while/body/eval_jaxpr/psum | solution.py:44
  771.2 75.9 %all-reduce.9.cloned.1.call-done = f32[123,64,50]{0,2,1:T(8,128)} async-done(((f32[123,64,50]{0,2,1:T(8,128)}), f32[123,64,50]{0,2,1:T(8,128)}) %all-reduce.9.cloned.1.call-update) | async-done | bytes 1574416 | tf_op jit(solution)/shard_map/while/body/eval_jaxpr/psum | solution.py:44
  922.7 64.9 %psum.57 = f32[64,50]{1,0:T(8,128)S(1)} all-reduce(f32[64,50]{1,0:T(8,128)S(1)} %reduce_sum.129), channel_id=1, replica_groups=mesh['parts'=1,'data'=128] {'data'}, use_global_device_ids=true, to_apply=%region_8.0 | all-reduce | flops 3200 | bytes 25600 | tf_op jit(solution)/shard_map/while/body/eval_jaxpr/psum | solution.py:44
  987.6 75.9 %all-reduce.9.cloned.1.call-done = f32[123,64,50]{0,2,1:T(8,128)} async-done(((f32[123,64,50]{0,2,1:T(8,128)}), f32[123,64,50]{0,2,1:T(8,128)}) %all-reduce.9.cloned.1.call-update) | async-done | bytes 1574416 | tf_op jit(solution)/shard_map/while/body/eval_jaxpr/psum | solution.py:44
  1139.0 64.9 %psum.57 = f32[64,50]{1,0:T(8,128)S(1)} all-reduce(f32[64,50]{1,0:T(8,128)S(1)} %reduce_sum.129), channel_id=1, replica_groups=mesh['parts'=1,'data'=128] {'data'}, use_global_device_ids=true, to_apply=%region_8.0 | all-reduce | flops 3200 | bytes 25600 | tf_op jit(solution)/shard_map/while/body/eval_jaxpr/psum | solution.py:44
  1203.9 75.9 %all-reduce.9.cloned.1.call-done = f32[123,64,50]{0,2,1:T(8,128)} async-done(((f32[123,64,50]{0,2,1:T(8,128)}), f32[123,64,50]{0,2,1:T(8,128)}) %all-reduce.9.cloned.1.call-update) | async-done | bytes 1574416 | tf_op jit(solution)/shard_map/while/body/eval_jaxpr/psum | solution.py:44
  1355.3 64.9 %psum.57 = f32[64,50]{1,0:T(8,128)S(1)} all-reduce(f32[64,50]{1,0:T(8,128)S(1)} %reduce_sum.129), channel_id=1, replica_groups=mesh['parts'=1,'data'=128] {'data'}, use_global_device_ids=true, to_apply=%region_8.0 | all-reduce | flops 3200 | bytes 25600 | tf_op jit(solution)/shard_map/while/body/eval_jaxpr/psum | solution.py:44
  1420.2 75.9 %all-reduce.9.cloned.1.call-done = f32[123,64,50]{0,2,1:T(8,128)} async-done(((f32[123,64,50]{0,2,1:T(8,128)}), f32[123,64,50]{0,2,1:T(8,128)}) %all-reduce.9.cloned.1.call-update) | async-done | bytes 1574416 | tf_op jit(solution)/shard_map/while/body/eval_jaxpr/psum | solution.py:44
  1571.7 64.9 %psum.57 = f32[64,50]{1,0:T(8,128)S(1)} all-reduce(f32[64,50]{1,0:T(8,128)S(1)} %reduce_sum.129), channel_id=1, replica_groups=mesh['parts'=1,'data'=128] {'data'}, use_global_device_ids=true, to_apply=%region_8.0 | all-reduce | flops 3200 | bytes 25600 | tf_op jit(solution)/shard_map/while/body/eval_jaxpr/psum | solution.py:44
  1636.6 75.9 %all-reduce.9.cloned.1.call-done = f32[123,64,50]{0,2,1:T(8,128)} async-done(((f32[123,64,50]{0,2,1:T(8,128)}), f32[123,64,50]{0,2,1:T(8,128)}) %all-reduce.9.cloned.1.call-update) | async-done | bytes 1574416 | tf_op jit(solution)/shard_map/while/body/eval_jaxpr/psum | solution.py:44
  1788.0 64.9 %psum.57 = f32[64,50]{1,0:T(8,128)S(1)} all-reduce(f32[64,50]{1,0:T(8,128)S(1)} %reduce_sum.129), channel_id=1, replica_groups=mesh['parts'=1,'data'=128] {'data'}, use_global_device_ids=true, to_apply=%region_8.0 | all-reduce | flops 3200 | bytes 25600 | tf_op jit(solution)/shard_map/while/body/eval_jaxpr/psum | solution.py:44
  1852.9 75.9 %all-reduce.9.cloned.1.call-done = f32[123,64,50]{0,2,1:T(8,128)} async-done(((f32[123,64,50]{0,2,1:T(8,128)}), f32[123,64,50]{0,2,1:T(8,128)}) %all-reduce.9.cloned.1.call-update) | async-done | bytes 1574416 | tf_op jit(solution)/shard_map/while/body/eval_jaxpr/psum | solution.py:44
  2004.3 64.9 %psum.57 = f32[64,50]{1,0:T(8,128)S(1)} all-reduce(f32[64,50]{1,0:T(8,128)S(1)} %reduce_sum.129), channel_id=1, replica_groups=mesh['parts'=1,'data'=128] {'data'}, use_global_device_ids=true, to_apply=%region_8.0 | all-reduce | flops 3200 | bytes 25600 | tf_op jit(solution)/shard_map/while/body/eval_jaxpr/psum | solution.py:44
  2069.2 75.9 %all-reduce.9.cloned.1.call-done = f32[123,64,50]{0,2,1:T(8,128)} async-done(((f32[123,64,50]{0,2,1:T(8,128)}), f32[123,64,50]{0,2,1:T(8,128)}) %all-reduce.9.cloned.1.call-update) | async-done | bytes 1574416 | tf_op jit(solution)/shard_map/while/body/eval_jaxpr/psum | solution.py:44
  2220.7 64.9 %psum.57 = f32[64,50]{1,0:T(8,128)S(1)} all-reduce(f32[64,50]{1,0:T(8,128)S(1)} %reduce_sum.129), channel_id=1, replica_groups=mesh['parts'=1,'data'=128] {'data'}, use_global_device_ids=true, to_apply=%region_8.0 | all-reduce | flops 3200 | bytes 25600 | tf_op jit(solution)/shard_map/while/body/eval_jaxpr/psum | solution.py:44
  2285.6 75.9 %all-reduce.9.cloned.1.call-done = f32[123,64,50]{0,2,1:T(8,128)} async-done(((f32[123,64,50]{0,2,1:T(8,128)}), f32[123,64,50]{0,2,1:T(8,128)}) %all-reduce.9.cloned.1.call-update) | async-done | bytes 1574416 | tf_op jit(solution)/shard_map/while/body/eval_jaxpr/psum | solution.py:44
  2437.0 64.9 %psum.57 = f32[64,50]{1,0:T(8,128)S(1)} all-reduce(f32[64,50]{1,0:T(8,128)S(1)} %reduce_sum.129), channel_id=1, replica_groups=mesh['parts'=1,'data'=128] {'data'}, use_global_device_ids=true, to_apply=%region_8.0 | all-reduce | flops 3200 | bytes 25600 | tf_op jit(solution)/shard_map/while/body/eval_jaxpr/psum | solution.py:44
  2501.9 75.9 %all-reduce.9.cloned.1.call-done = f32[123,64,50]{0,2,1:T(8,128)} async-done(((f32[123,64,50]{0,2,1:T(8,128)}), f32[123,64,50]{0,2,1:T(8,128)}) %all-reduce.9.cloned.1.call-update) | async-done | bytes 1574416 | tf_op jit(solution)/shard_map/while/body/eval_jaxpr/psum | solution.py:44
  2653.3 64.9 %psum.57 = f32[64,50]{1,0:T(8,128)S(1)} all-reduce(f32[64,50]{1,0:T(8,128)S(1)} %reduce_sum.129), channel_id=1, replica_groups=mesh['parts'=1,'data'=128] {'data'}, use_global_device_ids=true, to_apply=%region_8.0 | all-reduce | flops 3200 | bytes 25600 | tf_op jit(solution)/shard_map/while/body/eval_jaxpr/psum | solution.py:44
  2718.2 75.9 %all-reduce.9.cloned.1.call-done = f32[123,64,50]{0,2,1:T(8,128)} async-done(((f32[123,64,50]{0,2,1:T(8,128)}), f32[123,64,50]{0,2,1:T(8,128)}) %all-reduce.9.cloned.1.call-update) | async-done | bytes 1574416 | tf_op jit(solution)/shard_map/while/body/eval_jaxpr/psum | solution.py:44
  2869.7 64.9 %psum.57 = f32[64,50]{1,0:T(8,128)S(1)} all-reduce(f32[64,50]{1,0:T(8,128)S(1)} %reduce_sum.129), channel_id=1, replica_groups=mesh['parts'=1,'data'=128] {'data'}, use_global_device_ids=true, to_apply=%region_8.0 | all-reduce | flops 3200 | bytes 25600 | tf_op jit(solution)/shard_map/while/body/eval_jaxpr/psum | solution.py:44
  2934.6 75.9 %all-reduce.9.cloned.1.call-done = f32[123,64,50]{0,2,1:T(8,128)} async-done(((f32[123,64,50]{0,2,1:T(8,128)}), f32[123,64,50]{0,2,1:T(8,128)}) %all-reduce.9.cloned.1.call-update) | async-done | bytes 1574416 | tf_op jit(solution)/shard_map/while/body/eval_jaxpr/psum | solution.py:44
  3086.0 64.9 %psum.57 = f32[64,50]{1,0:T(8,128)S(1)} all-reduce(f32[64,50]{1,0:T(8,128)S(1)} %reduce_sum.129), channel_id=1, replica_groups=mesh['parts'=1,'data'=128] {'data'}, use_global_device_ids=true, to_apply=%region_8.0 | all-reduce | flops 3200 | bytes 25600 | tf_op jit(solution)/shard_map/while/body/eval_jaxpr/psum | solution.py:44
  3150.9 75.9 %all-reduce.9.cloned.1.call-done = f32[123,64,50]{0,2,1:T(8,128)} async-done(((f32[123,64,50]{0,2,1:T(8,128)}), f32[123,64,50]{0,2,1:T(8,128)}) %all-reduce.9.cloned.1.call-update) | async-done | bytes 1574416 | tf_op jit(solution)/shard_map/while/body/eval_jaxpr/psum | solution.py:44
  3302.3 64.9 %psum.57 = f32[64,50]{1,0:T(8,128)S(1)} all-reduce(f32[64,50]{1,0:T(8,128)S(1)} %reduce_sum.129), channel_id=1, replica_groups=mesh['parts'=1,'data'=128] {'data'}, use_global_device_ids=true, to_apply=%region_8.0 | all-reduce | flops 3200 | bytes 25600 | tf_op jit(solution)/shard_map/while/body/eval_jaxpr/psum | solution.py:44
  3367.2 75.9 %all-reduce.9.cloned.1.call-done = f32[123,64,50]{0,2,1:T(8,128)} async-done(((f32[123,64,50]{0,2,1:T(8,128)}), f32[123,64,50]{0,2,1:T(8,128)}) %all-reduce.9.cloned.1.call-update) | async-done | bytes 1574416 | tf_op jit(solution)/shard_map/while/body/eval_jaxpr/psum | solution.py:44
  3598.3 75.2 %all-reduce.7.cloned.1.call-done = f32[123,64,50]{0,2,1:T(8,128)} async-done(((f32[123,64,50]{0,2,1:T(8,128)}), f32[123,64,50]{0,2,1:T(8,128)}) %all-reduce.7.cloned.1.call-update) | async-done | bytes 1574416 | tf_op jit(solution)/shard_map/psum | solution.py:44
  (357 shorter events, 1456.9 us)
Async XLA Ops:
  7.2 188.5 %all-reduce.5.cloned.1.call-start = ((), (), s32[]{:S(2)}) async-start(), calls=%async_computation | async-start | bytes 3670016 | tf_op jit(solution)/shard_map/psum | solution.py:44
  201.5 213.1 %all-reduce.9.cloned.1.call-start = ((), (), s32[]{:S(2)}) async-start(), calls=%async_computation.2 | async-start | bytes 3670016 | tf_op jit(solution)/shard_map/while/body/eval_jaxpr/psum | solution.py:44
  273.6 144.2 %copy-start.1 = (bf16[1024,123]{1,0:T(8,128)(2,1)S(1)}, bf16[1024,123]{1,0:T(8,128)(2,1)}, u32[]{:S(2)}) copy-start(bf16[1024,123]{1,0:T(8,128)(2,1)} %get-tuple-element.198) | copy-start | bytes 755716 | tf_op jit(solution)/shard_map/while
  417.8 213.1 %all-reduce.9.cloned.1.call-start = ((), (), s32[]{:S(2)}) async-start(), calls=%async_computation.2 | async-start | bytes 3670016 | tf_op jit(solution)/shard_map/while/body/eval_jaxpr/psum | solution.py:44
  489.9 144.1 %copy-start.1 = (bf16[1024,123]{1,0:T(8,128)(2,1)S(1)}, bf16[1024,123]{1,0:T(8,128)(2,1)}, u32[]{:S(2)}) copy-start(bf16[1024,123]{1,0:T(8,128)(2,1)} %get-tuple-element.198) | copy-start | bytes 755716 | tf_op jit(solution)/shard_map/while
  634.1 213.1 %all-reduce.9.cloned.1.call-start = ((), (), s32[]{:S(2)}) async-start(), calls=%async_computation.2 | async-start | bytes 3670016 | tf_op jit(solution)/shard_map/while/body/eval_jaxpr/psum | solution.py:44
  706.2 144.2 %copy-start.1 = (bf16[1024,123]{1,0:T(8,128)(2,1)S(1)}, bf16[1024,123]{1,0:T(8,128)(2,1)}, u32[]{:S(2)}) copy-start(bf16[1024,123]{1,0:T(8,128)(2,1)} %get-tuple-element.198) | copy-start | bytes 755716 | tf_op jit(solution)/shard_map/while
  850.4 213.1 %all-reduce.9.cloned.1.call-start = ((), (), s32[]{:S(2)}) async-start(), calls=%async_computation.2 | async-start | bytes 3670016 | tf_op jit(solution)/shard_map/while/body/eval_jaxpr/psum | solution.py:44
  922.5 144.2 %copy-start.1 = (bf16[1024,123]{1,0:T(8,128)(2,1)S(1)}, bf16[1024,123]{1,0:T(8,128)(2,1)}, u32[]{:S(2)}) copy-start(bf16[1024,123]{1,0:T(8,128)(2,1)} %get-tuple-element.198) | copy-start | bytes 755716 | tf_op jit(solution)/shard_map/while
  1066.7 213.1 %all-reduce.9.cloned.1.call-start = ((), (), s32[]{:S(2)}) async-start(), calls=%async_computation.2 | async-start | bytes 3670016 | tf_op jit(solution)/shard_map/while/body/eval_jaxpr/psum | solution.py:44
  1138.9 144.2 %copy-start.1 = (bf16[1024,123]{1,0:T(8,128)(2,1)S(1)}, bf16[1024,123]{1,0:T(8,128)(2,1)}, u32[]{:S(2)}) copy-start(bf16[1024,123]{1,0:T(8,128)(2,1)} %get-tuple-element.198) | copy-start | bytes 755716 | tf_op jit(solution)/shard_map/while
  1283.1 213.1 %all-reduce.9.cloned.1.call-start = ((), (), s32[]{:S(2)}) async-start(), calls=%async_computation.2 | async-start | bytes 3670016 | tf_op jit(solution)/shard_map/while/body/eval_jaxpr/psum | solution.py:44
  1355.2 144.2 %copy-start.1 = (bf16[1024,123]{1,0:T(8,128)(2,1)S(1)}, bf16[1024,123]{1,0:T(8,128)(2,1)}, u32[]{:S(2)}) copy-start(bf16[1024,123]{1,0:T(8,128)(2,1)} %get-tuple-element.198) | copy-start | bytes 755716 | tf_op jit(solution)/shard_map/while
  1499.4 213.1 %all-reduce.9.cloned.1.call-start = ((), (), s32[]{:S(2)}) async-start(), calls=%async_computation.2 | async-start | bytes 3670016 | tf_op jit(solution)/shard_map/while/body/eval_jaxpr/psum | solution.py:44
  1571.5 144.2 %copy-start.1 = (bf16[1024,123]{1,0:T(8,128)(2,1)S(1)}, bf16[1024,123]{1,0:T(8,128)(2,1)}, u32[]{:S(2)}) copy-start(bf16[1024,123]{1,0:T(8,128)(2,1)} %get-tuple-element.198) | copy-start | bytes 755716 | tf_op jit(solution)/shard_map/while
  1715.7 213.1 %all-reduce.9.cloned.1.call-start = ((), (), s32[]{:S(2)}) async-start(), calls=%async_computation.2 | async-start | bytes 3670016 | tf_op jit(solution)/shard_map/while/body/eval_jaxpr/psum | solution.py:44
  1787.9 144.2 %copy-start.1 = (bf16[1024,123]{1,0:T(8,128)(2,1)S(1)}, bf16[1024,123]{1,0:T(8,128)(2,1)}, u32[]{:S(2)}) copy-start(bf16[1024,123]{1,0:T(8,128)(2,1)} %get-tuple-element.198) | copy-start | bytes 755716 | tf_op jit(solution)/shard_map/while
  1932.1 213.1 %all-reduce.9.cloned.1.call-start = ((), (), s32[]{:S(2)}) async-start(), calls=%async_computation.2 | async-start | bytes 3670016 | tf_op jit(solution)/shard_map/while/body/eval_jaxpr/psum | solution.py:44
  2004.2 144.2 %copy-start.1 = (bf16[1024,123]{1,0:T(8,128)(2,1)S(1)}, bf16[1024,123]{1,0:T(8,128)(2,1)}, u32[]{:S(2)}) copy-start(bf16[1024,123]{1,0:T(8,128)(2,1)} %get-tuple-element.198) | copy-start | bytes 755716 | tf_op jit(solution)/shard_map/while
  2148.4 213.1 %all-reduce.9.cloned.1.call-start = ((), (), s32[]{:S(2)}) async-start(), calls=%async_computation.2 | async-start | bytes 3670016 | tf_op jit(solution)/shard_map/while/body/eval_jaxpr/psum | solution.py:44
  2220.5 144.2 %copy-start.1 = (bf16[1024,123]{1,0:T(8,128)(2,1)S(1)}, bf16[1024,123]{1,0:T(8,128)(2,1)}, u32[]{:S(2)}) copy-start(bf16[1024,123]{1,0:T(8,128)(2,1)} %get-tuple-element.198) | copy-start | bytes 755716 | tf_op jit(solution)/shard_map/while
  2364.7 213.1 %all-reduce.9.cloned.1.call-start = ((), (), s32[]{:S(2)}) async-start(), calls=%async_computation.2 | async-start | bytes 3670016 | tf_op jit(solution)/shard_map/while/body/eval_jaxpr/psum | solution.py:44
  2436.9 144.2 %copy-start.1 = (bf16[1024,123]{1,0:T(8,128)(2,1)S(1)}, bf16[1024,123]{1,0:T(8,128)(2,1)}, u32[]{:S(2)}) copy-start(bf16[1024,123]{1,0:T(8,128)(2,1)} %get-tuple-element.198) | copy-start | bytes 755716 | tf_op jit(solution)/shard_map/while
  2581.1 213.1 %all-reduce.9.cloned.1.call-start = ((), (), s32[]{:S(2)}) async-start(), calls=%async_computation.2 | async-start | bytes 3670016 | tf_op jit(solution)/shard_map/while/body/eval_jaxpr/psum | solution.py:44
  2653.2 144.2 %copy-start.1 = (bf16[1024,123]{1,0:T(8,128)(2,1)S(1)}, bf16[1024,123]{1,0:T(8,128)(2,1)}, u32[]{:S(2)}) copy-start(bf16[1024,123]{1,0:T(8,128)(2,1)} %get-tuple-element.198) | copy-start | bytes 755716 | tf_op jit(solution)/shard_map/while
  2797.4 213.1 %all-reduce.9.cloned.1.call-start = ((), (), s32[]{:S(2)}) async-start(), calls=%async_computation.2 | async-start | bytes 3670016 | tf_op jit(solution)/shard_map/while/body/eval_jaxpr/psum | solution.py:44
  2869.5 144.2 %copy-start.1 = (bf16[1024,123]{1,0:T(8,128)(2,1)S(1)}, bf16[1024,123]{1,0:T(8,128)(2,1)}, u32[]{:S(2)}) copy-start(bf16[1024,123]{1,0:T(8,128)(2,1)} %get-tuple-element.198) | copy-start | bytes 755716 | tf_op jit(solution)/shard_map/while
  3013.7 213.1 %all-reduce.9.cloned.1.call-start = ((), (), s32[]{:S(2)}) async-start(), calls=%async_computation.2 | async-start | bytes 3670016 | tf_op jit(solution)/shard_map/while/body/eval_jaxpr/psum | solution.py:44
  3085.9 144.2 %copy-start.1 = (bf16[1024,123]{1,0:T(8,128)(2,1)S(1)}, bf16[1024,123]{1,0:T(8,128)(2,1)}, u32[]{:S(2)}) copy-start(bf16[1024,123]{1,0:T(8,128)(2,1)} %get-tuple-element.198) | copy-start | bytes 755716 | tf_op jit(solution)/shard_map/while
  3230.1 213.1 %all-reduce.9.cloned.1.call-start = ((), (), s32[]{:S(2)}) async-start(), calls=%async_computation.2 | async-start | bytes 3670016 | tf_op jit(solution)/shard_map/while/body/eval_jaxpr/psum | solution.py:44
  3302.2 144.2 %copy-start.1 = (bf16[1024,123]{1,0:T(8,128)(2,1)S(1)}, bf16[1024,123]{1,0:T(8,128)(2,1)}, u32[]{:S(2)}) copy-start(bf16[1024,123]{1,0:T(8,128)(2,1)} %get-tuple-element.198) | copy-start | bytes 755716 | tf_op jit(solution)/shard_map/while
  3446.4 227.2 %all-reduce.7.cloned.1.call-start = ((), (), s32[]{:S(2)}) async-start(), calls=%async_computation.1 | async-start | bytes 3670016 | tf_op jit(solution)/shard_map/psum | solution.py:44
  (5 other events, 202.5 us)
Sparse Core Ops, SparseCore 0:
  40.5 155.0 all-reduce.4
  264.3 150.1 all-reduce.8
  480.6 150.1 all-reduce.8
  696.9 150.1 all-reduce.8
  913.3 150.1 all-reduce.8
  1129.6 150.1 all-reduce.8
  1345.9 150.1 all-reduce.8
  1562.3 150.1 all-reduce.8
  1778.6 150.1 all-reduce.8
  1994.9 150.1 all-reduce.8
  2211.3 150.1 all-reduce.8
  2427.6 150.1 all-reduce.8
  2643.9 150.1 all-reduce.8
  2860.2 150.1 all-reduce.8
  3076.6 150.1 all-reduce.8
  3292.9 150.1 all-reduce.8
  3523.4 150.1 all-reduce.6
where the time goes:
time: 3690 us; the launch traced here: 3680 us
  waiting for transfers between devices  1300 us (35%)
  blocking collectives  1110 us (30%)
  local copies, waits for them, and re-layouts  586 us (16%)
  other arithmetic  400 us (11%)
  matrix products  275 us (7%)
    psum x17, waiting for transfers between devices, log_post_grad(): grad_in, grad_out = lax.psum((grad_in, grad_out), 'data')  1300 us
    psum x17, blocking collectives, log_post_grad(): grad_in, grad_out = lax.psum((grad_in, grad_out), 'data')  1110 us
    mul x32, local copies, waits for them, and re-layouts, local_terms(): residual[:, :, None] * pos_out * (1.0 - hidden_act * hidden_act)  309 us
    tanh x16, local copies, waits for them, and re-layouts, local_terms(): hidden_act = jnp.tanh(pre_act)  197 us
    dot_general x17, matrix products, local_terms(): lax.dot_general(x_rows, back_grad.reshape(num_rows, num_chain * hidden),...  166 us
    reduce_sum x17, other arithmetic, local_terms(): grad_out = jnp.sum(hidden_act * residual[:, :, None], axis=0)  154 us
    reduce_sum x16, other arithmetic, local_terms(): logits = jnp.sum(hidden_act * pos_out, axis=-1)  118 us
    dot_general x17, matrix products, local_terms(): jnp.dot(x_rows, w_flat, preferred_element_type=jnp.float32)  109 us
  transfers between devices with their start and end apart: 17, of which 17 were waited for; matrix products, arithmetic and copies ran while one was open for 4% of the time, Pallas kernels for 0%

commit v1 on v0

v1 whole, which is shorter than its diff:
```python
import functools
import math

import jax
import jax.numpy as jnp
from jax import lax
from jax.experimental import pallas as pl
from jax.experimental.pallas import tpu as pltpu
from jax.sharding import PartitionSpec as P

LEAPS = 16
PRIOR_VAR = 1.0
SIDE = 4
BLOCKS = SIDE ** 3
HID = 56
LANES = 128
LAB = 123
LOSS = 124
OUT = 127
ROW_PIECES = ((0, 352, 176), (352, 336, 176), (688, 336, 176))
OUT_PIECES = ((0, 24, 16), (24, 16, 8), (40, 16, 8))


def torus_gather(buf, pieces, coords, device_at, send_sem, recv_sem, barrier=None):
    descs = []
    plus = lambda c, d: lax.rem(c + d + SIDE, SIDE)

    def view(p, where, part):
        start, size, first = pieces[p]
        lo, n = {0: (start, size), 1: (start, first), 2: (start + first, size - first)}[part]
        return buf.at[where[0], where[1], where[2], pl.ds(lo, n), :]

    def copy(p, where, part, axis, step, slot):
        to = list(coords)
        to[axis] = plus(to[axis], step)
        ref = view(p, where, part)
        return pltpu.make_async_remote_copy(
            src_ref=ref, dst_ref=ref, send_sem=send_sem.at[p, slot], recv_sem=recv_sem.at[p, slot],
            device_id={'data': device_at(to)}, device_id_type=pl.DeviceIdType.MESH)

    def send(p, where, part, axis, step, slot):
        c = copy(p, where, part, axis, step, slot)
        c.start()
        descs.append(c)

    def wait(p, where, part, axis, step, slot):
        copy(p, where, part, axis, step, slot).wait_recv()

    orders = [(p, (p + 1) % 3, (p + 2) % 3) for p in range(3)]
    OFFS = (0, -1, 1, 2)

    def at(p, off0, off1, off2):
        where = [None, None, None]
        for axis, off in zip(orders[p], (off0, off1, off2)):
            where[axis] = slice(None) if off is None else (coords[axis] if off == 0 else plus(coords[axis], off))
        return where

    def start_full(p, ph, own, base):
        axis = orders[p][ph]
        send(p, own, 0, axis, 1, base)
        send(p, own, 0, axis, -1, base + 1)

    def relay(p, ph, low, high, base):
        axis = orders[p][ph]
        wait(p, low, 0, axis, 1, base)
        send(p, low, 1, axis, 1, base + 2)
        wait(p, high, 0, axis, 1, base + 1)
        send(p, high, 2, axis, -1, base + 3)

    def finish(p, ph, far, base):
        axis = orders[p][ph]
        wait(p, far, 1, axis, 1, base + 2)
        wait(p, far, 2, axis, 1, base + 3)

    B1, B2, B3 = 0, 4, 20
    for p in range(3):
        start_full(p, 0, at(p, 0, 0, 0), B1)
    for p in range(3):
        start_full(p, 1, at(p, 0, 0, 0), B2)
    for p in range(3):
        relay(p, 0, at(p, -1, 0, 0), at(p, 1, 0, 0), B1)
        start_full(p, 1, at(p, -1, 0, 0), B2 + 4)
        start_full(p, 1, at(p, 1, 0, 0), B2 + 8)
    for p in range(3):
        finish(p, 0, at(p, 2, 0, 0), B1)
        start_full(p, 1, at(p, 2, 0, 0), B2 + 12)
        start_full(p, 2, at(p, None, 0, 0), B3)
    for q in range(4):
        for p in range(3):
            relay(p, 1, at(p, OFFS[q], -1, 0), at(p, OFFS[q], 1, 0), B2 + 4 * q)
    for p in range(3):
        start_full(p, 2, at(p, None, -1, 0), B3 + 4)
        start_full(p, 2, at(p, None, 1, 0), B3 + 8)
    for q in range(4):
        for p in range(3):
            finish(p, 1, at(p, OFFS[q], 2, 0), B2 + 4 * q)
    for p in range(3):
        start_full(p, 2, at(p, None, 2, 0), B3 + 12)
    for q in range(4):
        for p in range(3):
            relay(p, 2, at(p, None, OFFS[q], -1), at(p, None, OFFS[q], 1), B3 + 4 * q)
    for q in range(4):
        for p in range(3):
            finish(p, 2, at(p, None, OFFS[q], 2), B3 + 4 * q)
    return descs


def block_index(b):
    return b // (SIDE * SIDE), (b // SIDE) % SIDE, b % SIDE


def hmc_kernel(step_size, solo, x_ref, start_ref, all_ref, x_all, xt_all, y_all, z_all, w2_ref, wbd_ref, a0, a1, zp0, zp1,
               b0, b1, g_ref, pos_ref, vel_ref, snd, rcv, x_send, x_recv, o_send, o_recv, e_send, e_recv, s_send, s_recv, own_sem):
    half_step = 0.5 * step_size
    me = lax.axis_index('data')
    core = me % 2
    chip = me // 2
    coords = (chip // (SIDE * SIDE), (chip // SIDE) % SIDE, chip % SIDE)
    partner = me + 1 - 2 * core

    def device_at(c):
        return ((c[0] * SIDE + c[1]) * SIDE + c[2]) * 2 + core

    own = pltpu.make_async_copy(x_ref, x_all.at[coords[0], coords[1], coords[2]], own_sem)
    own.start()
    if not solo:
        barrier = pltpu.get_barrier_semaphore()
        for axis in range(3):
            for step in (1, -1):
                to = list(coords)
                to[axis] = lax.rem(to[axis] + step + SIDE, SIDE)
                pl.semaphore_signal(barrier, inc=1, device_id={'data': device_at(to)}, device_id_type=pl.DeviceIdType.MESH)
        pl.semaphore_signal(barrier, inc=1, device_id={'data': partner}, device_id_type=pl.DeviceIdType.MESH)
        pl.semaphore_wait(barrier, 7)
    own.wait()
    if not solo:
        x_descs = torus_gather(x_all, ROW_PIECES, coords, device_at, x_send, x_recv)
        for d in x_descs:
            d.wait_send()

    def turn(b, carry):
        z, y, x = block_index(b)
        xt = x_all[z, y, x].T
        xt_all[b] = xt
        row = xt[112:128, :].astype(jnp.float32)[LAB - 112:LAB - 111, :]
        for k in range(8):
            y_all[b, k:k + 1, :] = row[:, k * LANES:(k + 1) * LANES]
        return carry

    lax.fori_loop(0, BLOCKS, turn, 0)

    pos_ref[...] = start_ref[0]
    vel_ref[...] = start_ref[1]
    lane = lax.broadcasted_iota(jnp.int32, (HID, LANES), 1)
    sub = lax.broadcasted_iota(jnp.int32, (HID, LANES), 0)
    is_param = (lane < LAB) | (lane == OUT)

    def forward(b, a_ref, zp_ref):
        xt = xt_all[b]
        pre = jnp.dot(wbd_ref[...], jnp.concatenate([xt[:, :512], xt[:, 512:]], axis=0), preferred_element_type=jnp.float32)
        act = jnp.tanh(pre)
        a_ref[...] = act
        w2 = w2_ref[...].reshape(HID // 8, 8, LANES)
        for k in range(8):
            s, j = k // 4, k % 4
            part = act[s * HID:(s + 1) * HID, j * LANES:(j + 1) * LANES].reshape(HID // 8, 8, LANES)
            zp_ref[8 * k:8 * k + 8, :] = jnp.sum(part * w2, axis=0)

    def backward(b, a_ref, zp_ref, b_ref, acc):
        z = zp_ref[pl.ds(0, 8, stride=8), :]
        for k in range(1, 8):
            z = z + zp_ref[pl.ds(k, 8, stride=8), :]
        z_all[b] = z
        res = y_all[b] - 1.0 / (1.0 + jnp.exp(-z))
        w2 = w2_ref[...]
        for j in range(4):
            parts = []
            for s in range(2):
                r = jnp.broadcast_to(res[4 * s + j:4 * s + j + 1, :], (HID, LANES))
                act = a_ref[s * HID:(s + 1) * HID, j * LANES:(j + 1) * LANES]
                ra = r * act
                acc = acc + ra
                parts.append((r - ra * act) * w2)
            b_ref[:, j * LANES:(j + 1) * LANES] = jnp.concatenate(parts, axis=0).astype(jnp.bfloat16)
        return acc

    def weight_grad(b, b_ref):
        z, y, x = block_index(b)
        rows = x_all[z, y, x]
        g_ref[...] += jnp.dot(b_ref[...], jnp.concatenate([rows[:512], rows[512:]], axis=1), preferred_element_type=jnp.float32)

    def leap(k, carry):
        pos = pos_ref[...] + jnp.where(k > 0, step_size, 0.0) * vel_ref[...]
        pos_ref[...] = pos
        w_in = jnp.where(lane < LAB, pos, 0.0)
        nil = jnp.zeros_like(w_in)
        wbd_ref[...] = jnp.concatenate([jnp.concatenate([w_in, nil], axis=1), jnp.concatenate([nil, w_in], axis=1)], axis=0).astype(jnp.bfloat16)
        w2_ref[...] = jnp.broadcast_to(pos[:, OUT:OUT + 1], (HID, LANES))
        g_ref[...] = jnp.zeros_like(g_ref)
        b1[...] = jnp.zeros_like(b1)
        forward(0, a0, zp0)

        def pair(i, acc):
            forward(2 * i + 1, a1, zp1)
            acc = backward(2 * i, a0, zp0, b0, acc)
            weight_grad(jnp.maximum(2 * i - 1, 0), b1)
            forward(jnp.minimum(2 * i + 2, BLOCKS - 1), a0, zp0)
            acc = backward(2 * i + 1, a1, zp1, b1, acc)
            weight_grad(2 * i, b0)
            return acc

        acc = lax.fori_loop(0, BLOCKS // 2, pair, jnp.zeros((HID, LANES), jnp.float32))
        weight_grad(BLOCKS - 1, b1)
        grad = g_ref[:HID, :LANES] + g_ref[HID:, LANES:]
        grad = jnp.where(lane < LAB, grad, jnp.where(lane == OUT, jnp.sum(acc, axis=1, keepdims=True), 0.0))
        slot = k % 2
        snd[slot] = grad

        @pl.when(k == LEAPS)
        def _():
            def loss_block(b, total):
                z = z_all[b]
                return total + (jnp.maximum(z, 0.0) + jnp.log1p(jnp.exp(-jnp.abs(z))) - y_all[b] * z)

            total = lax.fori_loop(0, BLOCKS, loss_block, jnp.zeros((8, LANES), jnp.float32))
            total = jnp.sum(jnp.sum(total, axis=1, keepdims=True), axis=0, keepdims=True)
            snd[slot] = jnp.where((lane == LOSS) & (sub == 0), total, grad)

        if not solo:
            ex = pltpu.make_async_remote_copy(
                src_ref=snd.at[slot], dst_ref=rcv.at[slot], send_sem=e_send, recv_sem=e_recv.at[slot],
                device_id={'data': partner}, device_id_type=pl.DeviceIdType.MESH)
            ex.start()
            ex.wait()
        total = snd[slot] + rcv[slot]
        rate = jnp.where((k == 0) | (k == LEAPS), half_step, step_size)
        vel_ref[...] += rate * jnp.where(is_param, total - pos * (1.0 / PRIOR_VAR), 0.0)
        return carry

    lax.fori_loop(0, LEAPS + 1, leap, 0)

    last = LEAPS % 2
    loss = snd[last][:1, LOSS:LOSS + 1] + rcv[last][:1, LOSS:LOSS + 1]
    pos = pos_ref[...]
    vel = vel_ref[...]
    square = (pos * pos) * (1.0 / (2.0 * PRIOR_VAR)) + 0.5 * (vel * vel)
    energy = loss + jnp.sum(jnp.sum(square, axis=1, keepdims=True), axis=0, keepdims=True)
    pos_out = jnp.where((lane == LOSS) & (sub == 0), energy, pos)
    if solo:
        all_ref[0, 0, 0, 0] = pos_out
        all_ref[1, 0, 0, 0] = vel
        return
    all_ref[core, coords[0], coords[1], coords[2]] = jnp.where(core == 0, pos_out, vel)
    o_descs = torus_gather(all_ref.at[core], OUT_PIECES, coords, device_at, o_send, o_recv)
    swap = pltpu.make_async_remote_copy(
        src_ref=all_ref.at[core], dst_ref=all_ref.at[core], send_sem=s_send, recv_sem=s_recv,
        device_id={'data': partner}, device_id_type=pl.DeviceIdType.MESH)
    swap.start()
    for d in o_descs:
        d.wait_send()
    swap.wait_send()
    pltpu.make_async_remote_copy(
        src_ref=all_ref.at[1 - core], dst_ref=all_ref.at[1 - core], send_sem=s_send, recv_sem=s_recv,
        device_id={'data': partner}, device_id_type=pl.DeviceIdType.MESH).wait_recv()


def call_kernel(x_pad, start, step_size, solo=False):
    rows = x_pad.shape[0]
    f32, bf16 = jnp.float32, jnp.bfloat16
    dma = pltpu.SemaphoreType.DMA
    return pl.pallas_call(
        functools.partial(hmc_kernel, step_size, solo),
        out_shape=jax.ShapeDtypeStruct((2, SIDE, SIDE, SIDE, HID, LANES), f32),
        in_specs=[pl.BlockSpec(memory_space=pl.ANY), pl.BlockSpec(memory_space=pltpu.VMEM)],
        out_specs=pl.BlockSpec(memory_space=pltpu.VMEM),
        scratch_shapes=[
            pltpu.VMEM((SIDE, SIDE, SIDE, rows, LANES), bf16),
            pltpu.VMEM((BLOCKS, LANES, rows), bf16),
            pltpu.VMEM((BLOCKS, 8, LANES), f32),
            pltpu.VMEM((BLOCKS, 8, LANES), f32),
            pltpu.VMEM((HID, LANES), f32),
            pltpu.VMEM((2 * HID, 2 * LANES), bf16),
            pltpu.VMEM((2 * HID, 512), f32),
            pltpu.VMEM((2 * HID, 512), f32),
            pltpu.VMEM((64, LANES), f32),
            pltpu.VMEM((64, LANES), f32),
            pltpu.VMEM((2 * HID, 512), bf16),
            pltpu.VMEM((2 * HID, 512), bf16),
            pltpu.VMEM((2 * HID, 2 * LANES), f32),
            pltpu.VMEM((HID, LANES), f32),
            pltpu.VMEM((HID, LANES), f32),
            pltpu.VMEM((2, HID, LANES), f32),
            pltpu.VMEM((2, HID, LANES), f32),
            dma((3, 36)), dma((3, 36)), dma((3, 36)), dma((3, 36)), dma, dma((2,)), dma, dma, dma,
        ],
        compiler_params=pltpu.CompilerParams(
            vmem_limit_bytes=60 * 2 ** 20, **({} if solo else dict(collective_id=0, has_side_effects=True))),
        name='hmc',
    )(x_pad, start)


def solution(mesh):
    row_spec = P('data', None)
    label_spec = P('data')
    in_spec = P(None, 'parts', None)
    out_spec = P('parts', None)
    chain_spec = P('parts')

    def run_chains(feats, labels, w_in, w_out, mom_in, mom_out):
        num_rows, num_feat = feats.shape
        hidden = w_in.shape[2]
        step_size = 1.0 / math.sqrt(num_rows * (num_feat + hidden))

        def device_body(x_rows, y_rows, pos_in, pos_out, vel_in, vel_out):
            x_pad = jnp.concatenate([x_rows, y_rows.astype(jnp.bfloat16)[:, None]], axis=1)
            x_pad = jnp.pad(x_pad, ((0, 0), (0, LANES - num_feat - 1)))
            chain = lax.axis_index('data') // 2

            def pack(arr_in, arr_out):
                mine_in = lax.dynamic_slice_in_dim(arr_in, chain, 1, axis=1)[:, 0, :]
                mine_out = lax.dynamic_slice_in_dim(arr_out, chain, 1, axis=0)
                both = jnp.concatenate([mine_in, jnp.zeros((OUT - num_feat, hidden), jnp.float32), mine_out], axis=0)
                return jnp.pad(both.T, ((0, HID - hidden), (0, 0)))

            start = jnp.stack([pack(pos_in, pos_out), pack(vel_in, vel_out)])
            every = call_kernel(x_pad, start, step_size).reshape(2, BLOCKS, HID, LANES)
            whole = jnp.transpose(every[:, :, :hidden, :], (0, 3, 1, 2))
            return (whole[0, :num_feat], whole[0, OUT], whole[1, :num_feat], whole[1, OUT], every[0, :, 0, LOSS])

        mapped = jax.shard_map(device_body, mesh=mesh, in_specs=(row_spec, label_spec, in_spec, out_spec, in_spec, out_spec), out_specs=(in_spec, out_spec, in_spec, out_spec, chain_spec), check_vma=False)
        return mapped(feats, labels, w_in, w_out, mom_in, mom_out)

    return run_chains
```

time: 3690 us -> 339 us (0.09)
  waiting for transfers between devices: 1300 us -> 0 us
  blocking collectives: 1110 us -> 0 us
  local copies, waits for them, and re-layouts: 586 us -> 10.9 us
  other arithmetic: 400 us -> 3.24 us
  Pallas kernels: 0 us -> 323 us
  matrix products: 275 us -> 0 us
    psum x17 -> x0, waiting for transfers between devices: 1300 us -> none  [log_post_grad(): grad_in, grad_out = lax.psum((grad_in, grad_out), 'data')]
    psum x17 -> x0, blocking collectives: 1110 us -> none  [log_post_grad(): grad_in, grad_out = lax.psum((grad_in, grad_out), 'data')]
    pallas_call x0 -> x1, Pallas kernels: none -> 323 us  [call_kernel(): pl.pallas_call(functools.partial(hmc_kernel, step_size, solo), out_shape=...]
    mul x48 -> x0, local copies, waits for them, and re-layouts: 311 us -> none  [the longest x32 309 us: local_terms(): residual[:, :, None] * pos_out * (1.0 - hidden_act * hidden_act)]
    reduce_sum x38 -> x0, other arithmetic: 279 us -> none  [the longest x17 154 us: local_terms(): grad_out = jnp.sum(hidden_act * residual[:, :, None], axis=0)]
    dot_general x34 -> x0, matrix products: 275 us -> none  [the longest x17 166 us: local_terms(): lax.dot_general(x_rows, back_grad.reshape(num_rows, num_chain * hidden),...]
    tanh x16 -> x0, local copies, waits for them, and re-layouts: 197 us -> none  [local_terms(): hidden_act = jnp.tanh(pre_act)]
    reshape x35 -> x0, local copies, waits for them, and re-layouts: 64.7 us -> none  [the longest x17 31.9 us: log_post_grad(): w_flat = pos_in.astype(jnp.bfloat16).reshape(num_feat, num_chain * hidden)]
  transfers between devices with their start and end apart: 17 -> 0, of which waited for: 17 -> 0; matrix products, arithmetic and copies ran while one was open for 4% -> 0% of each run, Pallas kernels for 0% -> 0%
where the time goes in v1:
time: 339 us; the launch traced here: 338 us
  Pallas kernels  323 us (95%)
  local copies, waits for them, and re-layouts  10.9 us (3%)
    pallas_call x1, Pallas kernels, call_kernel(): pl.pallas_call(functools.partial(hmc_kernel, step_size, solo), out_shape=...  323 us

profile of v1, /device:TPU:1, one launch (start us, length us, event | category | flops | bytes accessed | tf_op | source)
XLA Modules:
  0.0 338.2 jit_solution(12119423101388325061)
XLA Ops:
  0.7 0.1 pad.20.clone
  0.7 0.7 convert_element_type.8
  1.4 1.1 constant_dynamic-slice_fusion.1
  2.5 0.8 constant_dynamic-slice_fusion
  3.4 0.1 maximum_bitcast_fusion
  3.5 0.6 pad_maximum_fusion.start_ref
  4.1 0.2 broadcast_in_dim.4
  4.3 1.8 fusion.2.x_ref
  6.2 323.3 %hmc.1 = f32[2,4,4,4,56,128]{5,4,3,2,1,0:T(8,128)} custom-call(bf16[1024,128]{1,0:T(8,128)(2,1)} %fusion.2.x_ref, f32[2,56,128]{2,1,0:T(8,128)} %pad_maximum_fusion.start_ref), custom_call_target="tpu_custom_call" | custom-call | tf_op jit(solution)/shard_map/hmc/pallas_call | solution.py:271
  329.5 1.1 slice.29
  330.6 0.6 copy.26
  331.2 2.7 copy.30
  333.8 2.4 slice_reduce_fusion
  336.2 1.9 slice_bitcast_fusion
  (5 shorter events, 0.0 us)

commit v2 on v1

v2 whole, which is shorter than its diff:
```python
import functools
import math

import jax
import jax.numpy as jnp
from jax import lax
from jax.experimental import pallas as pl
from jax.experimental.pallas import tpu as pltpu
from jax.sharding import PartitionSpec as P

LEAPS = 16
PRIOR_VAR = 1.0
SIDE = 4
BLOCKS = SIDE ** 3
HID = 56
LANES = 128
LAB = 123
LOSS = 124
OUT = 127
UNIT = 8
ROW_PIECES = ((0, 352, 176), (352, 336, 176), (688, 336, 176))
OUT_PIECES = ((0, 24, 16), (24, 16, 8), (40, 16, 8))


def torus_gather(buf, pieces, coords, device_at, send_sem, recv_sem, near=None, middle=None):
    descs = []
    plus = lambda c, d: lax.rem(c + d + SIDE, SIDE)

    def view(p, where, part):
        start, size, first = pieces[p]
        lo, n = {0: (start, size), 1: (start, first), 2: (start + first, size - first)}[part]
        return buf.at[where[0], where[1], where[2], pl.ds(lo, n), :]

    def copy(p, where, part, axis, step, slot):
        to = list(coords)
        to[axis] = plus(to[axis], step)
        ref = view(p, where, part)
        return pltpu.make_async_remote_copy(
            src_ref=ref, dst_ref=ref, send_sem=send_sem.at[p, slot], recv_sem=recv_sem.at[p, slot],
            device_id={'data': device_at(to)}, device_id_type=pl.DeviceIdType.MESH)

    def send(p, where, part, axis, step, slot):
        c = copy(p, where, part, axis, step, slot)
        c.start()
        descs.append(c)

    def wait(p, where, part, axis, step, slot):
        copy(p, where, part, axis, step, slot).wait_recv()

    orders = [(p, (p + 1) % 3, (p + 2) % 3) for p in range(3)]
    OFFS = (0, -1, 1, 2)

    def at(p, off0, off1, off2):
        where = [None, None, None]
        for axis, off in zip(orders[p], (off0, off1, off2)):
            where[axis] = slice(None) if off is None else (coords[axis] if off == 0 else plus(coords[axis], off))
        return where

    def start_full(p, ph, own, base):
        axis = orders[p][ph]
        send(p, own, 0, axis, 1, base)
        send(p, own, 0, axis, -1, base + 1)

    def relay(p, ph, low, high, base):
        axis = orders[p][ph]
        wait(p, low, 0, axis, 1, base)
        send(p, low, 1, axis, 1, base + 2)
        wait(p, high, 0, axis, 1, base + 1)
        send(p, high, 2, axis, -1, base + 3)

    def finish(p, ph, far, base):
        axis = orders[p][ph]
        wait(p, far, 1, axis, 1, base + 2)
        wait(p, far, 2, axis, 1, base + 3)

    B1, B2, B3 = 0, 4, 20
    for p in range(3):
        start_full(p, 0, at(p, 0, 0, 0), B1)
    for p in range(3):
        start_full(p, 1, at(p, 0, 0, 0), B2)
    for p in range(3):
        relay(p, 0, at(p, -1, 0, 0), at(p, 1, 0, 0), B1)
        start_full(p, 1, at(p, -1, 0, 0), B2 + 4)
        start_full(p, 1, at(p, 1, 0, 0), B2 + 8)
    for p in range(3):
        finish(p, 0, at(p, 2, 0, 0), B1)
        start_full(p, 1, at(p, 2, 0, 0), B2 + 12)
        start_full(p, 2, at(p, None, 0, 0), B3)
    for q in range(4):
        for p in range(3):
            relay(p, 1, at(p, OFFS[q], -1, 0), at(p, OFFS[q], 1, 0), B2 + 4 * q)
    for p in range(3):
        start_full(p, 2, at(p, None, -1, 0), B3 + 4)
        start_full(p, 2, at(p, None, 1, 0), B3 + 8)
    for q in range(4):
        for p in range(3):
            finish(p, 1, at(p, OFFS[q], 2, 0), B2 + 4 * q)
    for p in range(3):
        start_full(p, 2, at(p, None, 2, 0), B3 + 12)
    for q in range(4):
        for p in range(3):
            relay(p, 2, at(p, None, OFFS[q], -1), at(p, None, OFFS[q], 1), B3 + 4 * q)
    if near is not None:
        near()
    for q in range(4):
        if q == 3 and middle is not None:
            middle()
        for p in range(3):
            finish(p, 2, at(p, None, OFFS[q], 2), B3 + 4 * q)
    return descs


def block_index(b):
    return b // (SIDE * SIDE), (b // SIDE) % SIDE, b % SIDE


def hmc_kernel(step_size, solo, feat_ref, lab_ref, w_ref, wo_ref, m_ref, mo_ref, w_end, wo_end, m_end, mo_end, e_end,
               x_in, w_tmp, x_all, xt_all, y_all, z_all, w2_ref, wbd_ref, a_ref, zp_ref,
               b_ref, g_ref, pos_ref, vel_ref, snd, rcv, all_ref, x_send, x_recv, o_send, o_recv, e_send, e_recv, s_send, s_recv, own_sem):
    half_step = 0.5 * step_size
    num_feat = feat_ref.shape[1]
    hidden = w_ref.shape[0]
    me = lax.axis_index('data')
    core = me % 2
    chip = me // 2
    coords = (chip // (SIDE * SIDE), (chip // SIDE) % SIDE, chip % SIDE)
    partner = me + 1 - 2 * core

    def device_at(c):
        return ((c[0] * SIDE + c[1]) * SIDE + c[2]) * 2 + core

    loads = [pltpu.make_async_copy(feat_ref, x_in, own_sem.at[0])]
    eight = pl.multiple_of((chip // 8) * 8, 8)
    for n, ref in enumerate((w_ref, m_ref)):
        loads.append(pltpu.make_async_copy(ref.at[:, pl.ds(eight, 8), :], w_tmp.at[n], own_sem.at[n + 1]))
    for load in loads:
        load.start()
    if not solo:
        barrier = pltpu.get_barrier_semaphore()
        for axis in range(3):
            for step in (1, -1):
                to = list(coords)
                to[axis] = lax.rem(to[axis] + step + SIDE, SIDE)
                pl.semaphore_signal(barrier, inc=1, device_id={'data': device_at(to)}, device_id_type=pl.DeviceIdType.MESH)
        pl.semaphore_signal(barrier, inc=1, device_id={'data': partner}, device_id_type=pl.DeviceIdType.MESH)
    labels = lab_ref[...].astype(jnp.float32)
    loads[0].wait()
    for k in range(8):
        column = jnp.broadcast_to(labels[k:k + 1, :], (LANES, LANES)).T
        spare = lax.broadcasted_iota(jnp.int32, (LANES, LANES), 1)
        rows = pl.ds(k * LANES, LANES)
        x_all[coords[0], coords[1], coords[2], rows, :] = jnp.where(spare == LAB, column, 0.0).astype(jnp.bfloat16)
        x_all[coords[0], coords[1], coords[2], rows, :num_feat] = x_in[rows, :]
    if not solo:
        pl.semaphore_wait(barrier, 7)

    def turn(where):
        z, y, x = where
        b = (z * SIDE + y) * SIDE + x
        for k in range(8):
            xt = x_all[z, y, x, k * LANES:(k + 1) * LANES, :].T
            xt_all[b, k] = xt
            y_all[b, k:k + 1, :] = xt[112:128, :].astype(jnp.float32)[LAB - 112:LAB - 111, :]

    def moved(offsets):
        return tuple(lax.rem(c + o, SIDE) for c, o in zip(coords, offsets))

    def three(i):
        return 3 + i

    def near():
        def body(i, carry):
            turn(moved((three(i // 9), three((i // 3) % 3), three(i % 3))))
            return carry
        lax.fori_loop(0, 27, body, 0)

    def middle():
        def body(i, carry):
            u, v = three(i // 3), three(i % 3)
            turn(moved((2, u, v)))
            turn(moved((u, 2, v)))
            turn(moved((u, v, 2)))
            return carry
        lax.fori_loop(0, 9, body, 0)

    def far():
        def body(i, carry):
            u = three(i)
            turn(moved((2, 2, u)))
            turn(moved((2, u, 2)))
            turn(moved((u, 2, 2)))
            return carry
        lax.fori_loop(0, 3, body, 0)
        turn(moved((2, 2, 2)))

    x_descs = []
    if solo:
        near()
        middle()
    else:
        x_descs = torus_gather(x_all, ROW_PIECES, coords, device_at, x_send, x_recv, near, middle)
    far()
    for d in x_descs:
        d.wait_send()
    pos_ref[...] = jnp.zeros_like(pos_ref)
    vel_ref[...] = jnp.zeros_like(vel_ref)
    chain_row = lax.broadcasted_iota(jnp.int32, (hidden, 8, num_feat), 1) == chip % 8
    chain_lane = lax.broadcasted_iota(jnp.int32, wo_ref.shape, 1) == chip
    for n, (ref, last) in enumerate(((pos_ref, wo_ref), (vel_ref, mo_ref))):
        loads[n + 1].wait()
        ref[:hidden, :num_feat] = jnp.sum(jnp.where(chain_row, w_tmp[n], 0.0), axis=1)
        ref[:hidden, OUT:OUT + 1] = jnp.sum(jnp.where(chain_lane, last[...], 0.0), axis=1, keepdims=True)

    lane = lax.broadcasted_iota(jnp.int32, (HID, LANES), 1)
    sub = lax.broadcasted_iota(jnp.int32, (HID, LANES), 0)
    is_param = (lane < LAB) | (lane == OUT)

    def forward(b):
        wbd = jnp.concatenate([wbd_ref[0], wbd_ref[1]], axis=1)
        pres = []
        for t in range(2):
            tiles = [jnp.concatenate([xt_all[b, 4 * s + 2 * t], xt_all[b, 4 * s + 2 * t + 1]], axis=1) for s in range(2)]
            pres.append(jnp.dot(wbd, jnp.concatenate(tiles, axis=0), preferred_element_type=jnp.float32))
        return pres

    def activate(pres, u):
        w2 = w2_ref[...].reshape(HID // 8, 8, LANES)
        for t in range(2):
            act = jnp.tanh(pres[t])
            for h in range(2):
                j = 2 * t + h
                a_ref[u, j] = act[:, h * LANES:(h + 1) * LANES]
                for s in range(2):
                    part = act[s * HID:(s + 1) * HID, h * LANES:(h + 1) * LANES].reshape(HID // 8, 8, LANES)
                    k = 4 * s + j
                    zp_ref[u, 8 * k:8 * k + 8, :] = jnp.sum(part * w2, axis=0)

    def backward(b, u, acc):
        z = zp_ref[u, pl.ds(0, 8, stride=8), :]
        for k in range(1, 8):
            z = z + zp_ref[u, pl.ds(k, 8, stride=8), :]
        z_all[b] = z
        res = y_all[b] - 1.0 / (1.0 + jnp.exp(-z))
        w2 = w2_ref[...]
        for j in range(4):
            parts = []
            for s in range(2):
                r = jnp.broadcast_to(res[4 * s + j:4 * s + j + 1, :], (HID, LANES))
                act = a_ref[u, j, s * HID:(s + 1) * HID, :]
                ra = r * act
                acc = acc + ra
                parts.append((r - ra * act) * w2)
            b_ref[u, j] = jnp.concatenate(parts, axis=0).astype(jnp.bfloat16)
        return acc

    def weight_grad(b, u):
        z, y, x = block_index(b)
        rows = x_all.at[z, y, x]
        lhs = jnp.concatenate([b_ref[u, j] for j in range(4)], axis=1)
        return jnp.dot(lhs, jnp.concatenate([rows[:512, :], rows[512:, :]], axis=1), preferred_element_type=jnp.float32)

    def leap(k, carry):
        pos = pos_ref[...] + jnp.where(k > 0, step_size, 0.0) * vel_ref[...]
        pos_ref[...] = pos
        w_in = jnp.where(lane < LAB, pos, 0.0)
        nil = jnp.zeros_like(w_in)
        wbd_ref[0] = jnp.concatenate([w_in, nil], axis=0).astype(jnp.bfloat16)
        wbd_ref[1] = jnp.concatenate([nil, w_in], axis=0).astype(jnp.bfloat16)
        w2_ref[...] = jnp.broadcast_to(pos[:, OUT:OUT + 1], (HID, LANES))
        g_ref[...] = jnp.zeros_like(g_ref)
        b_ref[...] = jnp.zeros_like(b_ref)
        for u in range(UNIT):
            activate(forward(u), u)

        def unit(i, acc):
            now = i * UNIT
            prior = jnp.maximum(now - UNIT, 0)
            ahead = jnp.minimum(now + UNIT, BLOCKS - UNIT)
            pres = [forward(ahead + u) for u in range(UNIT)]
            part = weight_grad(prior, 0)
            for u in range(1, UNIT):
                part = part + weight_grad(prior + u, u)
            for u in range(UNIT):
                acc = backward(now + u, u, acc)
            for u in range(UNIT):
                activate(pres[u], u)
            g_ref[...] += part
            return acc

        acc = lax.fori_loop(0, BLOCKS // UNIT, unit, jnp.zeros((HID, LANES), jnp.float32))
        for u in range(UNIT):
            g_ref[...] += weight_grad(BLOCKS - UNIT + u, u)
        grad = g_ref[:HID, :LANES] + g_ref[HID:, LANES:]
        grad = jnp.where(lane < LAB, grad, jnp.where(lane == OUT, jnp.sum(acc, axis=1, keepdims=True), 0.0))
        slot = k % 2
        snd[slot] = grad

        @pl.when(k == LEAPS)
        def _():
            def loss_block(b, total):
                z = z_all[b]
                return total + (jnp.maximum(z, 0.0) + jnp.log1p(jnp.exp(-jnp.abs(z))) - y_all[b] * z)

            total = lax.fori_loop(0, BLOCKS, loss_block, jnp.zeros((8, LANES), jnp.float32))
            total = jnp.sum(jnp.sum(total, axis=1, keepdims=True), axis=0, keepdims=True)
            snd[slot] = jnp.where((lane == LOSS) & (sub == 0), total, grad)

        if not solo:
            ex = pltpu.make_async_remote_copy(
                src_ref=snd.at[slot], dst_ref=rcv.at[slot], send_sem=e_send, recv_sem=e_recv.at[slot],
                device_id={'data': partner}, device_id_type=pl.DeviceIdType.MESH)
            ex.start()
            ex.wait()
        total = snd[slot] + rcv[slot]
        rate = jnp.where((k == 0) | (k == LEAPS), half_step, step_size)
        vel_ref[...] += rate * jnp.where(is_param, total - pos * (1.0 / PRIOR_VAR), 0.0)
        return carry

    lax.fori_loop(0, LEAPS + 1, leap, 0)

    last = LEAPS % 2
    loss = snd[last][:1, LOSS:LOSS + 1] + rcv[last][:1, LOSS:LOSS + 1]
    pos = pos_ref[...]
    vel = vel_ref[...]
    square = (pos * pos) * (1.0 / (2.0 * PRIOR_VAR)) + 0.5 * (vel * vel)
    energy = loss + jnp.sum(jnp.sum(square, axis=1, keepdims=True), axis=0, keepdims=True)
    tails = []
    for ref in (pos_ref, vel_ref):
        w2 = jnp.broadcast_to(ref[...][:, OUT:OUT + 1], (HID, LANES))
        row = jnp.concatenate([w2, jnp.zeros((LANES - HID, LANES), jnp.float32)], axis=0).T[:1, :]
        tails.append(jnp.broadcast_to(row, (HID, LANES)))
    tails[0] = jnp.where(lane == hidden, energy, tails[0])
    outs = [jnp.where(sub == hidden, t, v) for t, v in zip(tails, (pos, vel))]
    if solo:
        all_ref[0, 0, 0, 0] = outs[0]
        all_ref[1, 0, 0, 0] = outs[1]
    else:
        all_ref[core, coords[0], coords[1], coords[2]] = jnp.where(core == 0, outs[0], outs[1])
        o_descs = torus_gather(all_ref.at[core], OUT_PIECES, coords, device_at, o_send, o_recv)
        swap = pltpu.make_async_remote_copy(
            src_ref=all_ref.at[core], dst_ref=all_ref.at[core], send_sem=s_send, recv_sem=s_recv,
            device_id={'data': partner}, device_id_type=pl.DeviceIdType.MESH)
        swap.start()
        for d in o_descs:
            d.wait_send()
        swap.wait_send()
        pltpu.make_async_remote_copy(
            src_ref=all_ref.at[1 - core], dst_ref=all_ref.at[1 - core], send_sem=s_send, recv_sem=s_recv,
            device_id={'data': partner}, device_id_type=pl.DeviceIdType.MESH).wait_recv()

    flat = all_ref.reshape(2, BLOCKS * HID, LANES)

    def spread(h, carry):
        for n, ref in enumerate((w_end, m_end)):
            for c in range(0, BLOCKS, 8):
                ref[h, c:c + 8, :] = flat[n, pl.ds(c * HID + h, 8, stride=HID), :][:, :num_feat]
        return carry

    lax.fori_loop(0, hidden, spread, 0)
    for n, ref in enumerate((wo_end, mo_end)):
        tail = jnp.concatenate([flat[n, pl.ds(c * HID + hidden, 8, stride=HID), :] for c in range(0, BLOCKS, 8)]
                               + [jnp.zeros((LANES - BLOCKS, LANES), jnp.float32)], axis=0).T
        ref[...] = tail[:hidden, :BLOCKS]
        if n == 0:
            e_end[...] = tail[hidden:hidden + 1, :BLOCKS]


def call_kernel(feats, labels, w_in, w_out, mom_in, mom_out, step_size, solo=False):
    rows, num_feat = feats.shape
    hidden, chains, _ = w_in.shape
    f32, bf16 = jnp.float32, jnp.bfloat16
    dma = pltpu.SemaphoreType.DMA
    vmem = pl.BlockSpec(memory_space=pltpu.VMEM)
    hbm = pl.BlockSpec(memory_space=pl.ANY)
    return pl.pallas_call(
        functools.partial(hmc_kernel, step_size, solo),
        out_shape=[jax.ShapeDtypeStruct(w_in.shape, f32), jax.ShapeDtypeStruct(w_out.shape, f32)] * 2 + [jax.ShapeDtypeStruct((1, chains), f32)],
        in_specs=[hbm, vmem, hbm, vmem, hbm, vmem],
        out_specs=[vmem] * 5,
        scratch_shapes=[
            pltpu.VMEM((rows, num_feat), bf16),
            pltpu.VMEM((2, hidden, 8, num_feat), f32),
            pltpu.VMEM((SIDE, SIDE, SIDE, rows, LANES), bf16),
            pltpu.VMEM((BLOCKS, rows // LANES, LANES, LANES), bf16),
            pltpu.VMEM((BLOCKS, 8, LANES), f32),
            pltpu.VMEM((BLOCKS, 8, LANES), f32),
            pltpu.VMEM((HID, LANES), f32),
            pltpu.VMEM((2, 2 * HID, LANES), bf16),
            pltpu.VMEM((UNIT, 4, 2 * HID, LANES), f32),
            pltpu.VMEM((UNIT, 64, LANES), f32),
            pltpu.VMEM((UNIT, 4, 2 * HID, LANES), bf16),
            pltpu.VMEM((2 * HID, 2 * LANES), f32),
            pltpu.VMEM((HID, LANES), f32),
            pltpu.VMEM((HID, LANES), f32),
            pltpu.VMEM((2, HID, LANES), f32),
            pltpu.VMEM((2, HID, LANES), f32),
            pltpu.VMEM((2, SIDE, SIDE, SIDE, HID, LANES), f32),
            dma((3, 36)), dma((3, 36)), dma((3, 36)), dma((3, 36)), dma, dma((2,)), dma, dma, dma((3,)),
        ],
        compiler_params=pltpu.CompilerParams(
            vmem_limit_bytes=60 * 2 ** 20, **({} if solo else dict(collective_id=0, has_side_effects=True))),
        name='hmc',
    )(feats, labels, w_in, w_out, mom_in, mom_out)


def solution(mesh):
    row_spec = P('data', None)
    label_spec = P('data')
    in_spec = P(None, 'parts', None)
    out_spec = P('parts', None)
    chain_spec = P('parts')

    def run_chains(feats, labels, w_in, w_out, mom_in, mom_out):
        num_rows, num_feat = feats.shape
        hidden = w_in.shape[2]
        step_size = 1.0 / math.sqrt(num_rows * (num_feat + hidden))

        def device_body(x_rows, y_rows, pos_in, pos_out, vel_in, vel_out):
            turned = [jnp.transpose(v) for v in (pos_in, pos_out, vel_in, vel_out)]
            ends = call_kernel(x_rows, y_rows.reshape(8, LANES), *turned, step_size)
            return tuple(jnp.transpose(v) for v in ends[:4]) + (ends[4].reshape(-1),)

        mapped = jax.shard_map(device_body, mesh=mesh, in_specs=(row_spec, label_spec, in_spec, out_spec, in_spec, out_spec), out_specs=(in_spec, out_spec, in_spec, out_spec, chain_spec), check_vma=False)
        return mapped(feats, labels, w_in, w_out, mom_in, mom_out)

    return run_chains
```

time: 339 us -> 282 us (0.83)
  Pallas kernels: 323 us -> 275 us
  local copies, waits for them, and re-layouts: 10.9 us -> 5.82 us
    pallas_call x1, Pallas kernels: 323 us -> 275 us  [call_kernel(): pl.pallas_call(functools.partial(hmc_kernel, step_size, solo), out_shape=...]
    slice x2 -> x0, local copies, waits for them, and re-layouts: 3.46 us -> none  [the longest x1 2.39 us: device_body(): whole[1, OUT]]
where the time goes in v2:
time: 282 us
  Pallas kernels  275 us (98%)
  local copies, waits for them, and re-layouts  5.82 us (2%)
    pallas_call x1, Pallas kernels, call_kernel(): pl.pallas_call(functools.partial(hmc_kernel, step_size, solo), out_shape=...  275 us
    unnamed x13, local copies, waits for them, and re-layouts  5.82 us

profile of v2, /device:TPU:1, one launch (start us, length us, event | category | flops | bytes accessed | tf_op | source)
XLA Modules:
  0.0 281.5 jit_solution(9480571312839848456)
XLA Ops:
  0.6 275.0 %hmc.1 = (f32[50,64,123]{2,1,0:T(8,128)}, f32[50,64]{1,0:T(8,128)}, f32[50,64,123]{2,1,0:T(8,128)}, f32[50,64]{1,0:T(8,128)}, f32[1,64]{1,0:T(1,128)}) custom-call(bf16[1024,123]{1,0:T(8,128)(2,1)} %feat_ref.1, s32[8,128]{1,0:T(8,128)} %bitcast.18, f32[50,64,123]{2,1,0:T(8,128)} %bitcast.10, f32[50,64]{1,0:T(8,128)} %bitcast.16, f32[50,64,123]{2,1,0:T(8,128)} %bitcast.11, ...), custom_call_target="tpu_custom_call" | custom-call | tf_op jit(solution)/shard_map/hmc/pallas_call | solution.py:375
  275.7 0.0 copy-start.2
  275.7 0.0 copy-start
  275.7 2.9 %copy.16 = f32[123,64,50]{0,1,2:T(8,128)} copy(f32[123,64,50]{0,1,2:T(8,128)} %bitcast.13) | data formatting | bytes 3148800
  278.6 0.0 copy-done.2
  278.6 0.6 copy.17
  279.2 0.0 copy-done
  279.2 0.0 copy-start.1
  279.2 0.0 copy-start.3
  279.2 1.2 copy.18
  280.4 0.0 copy-done.1
  280.4 0.6 copy.19
  281.0 0.0 copy-done.3
  281.0 0.5 copy.20
Async XLA Ops:
  275.7 2.9 %copy-start.2 = (f32[50,64]{1,0:T(8,128)S(1)}, f32[50,64]{1,0:T(8,128)}, u32[]{:S(2)}) copy-start(f32[50,64]{1,0:T(8,128)} %get-tuple-element.11) | copy-start | bytes 38404
  275.7 3.5 %copy-start = (f32[50,64,123]{2,1,0:T(8,128)S(1)}, f32[50,64,123]{2,1,0:T(8,128)}, u32[]{:S(2)}) copy-start(f32[50,64,123]{2,1,0:T(8,128)} %get-tuple-element.12) | copy-start | bytes 4723204
  279.2 1.2 copy-start.1
  279.2 1.8 copy-start.3

commit v3 on v2

v3 whole, which is shorter than its diff:
```python
import functools
import math

import jax
import jax.numpy as jnp
from jax import lax
from jax.experimental import pallas as pl
from jax.experimental.pallas import tpu as pltpu
from jax.sharding import PartitionSpec as P

LEAPS = 16
PRIOR_VAR = 1.0
SIDE = 4
BLOCKS = SIDE ** 3
HID = 56
LANES = 128
LAB = 123
LOSS = 124
OUT = 127
UNROLL = 4
MIB = 2 ** 20
ROW_PIECES = ((0, 352, 176), (352, 336, 176), (688, 336, 176))
OUT_PIECES = ((0, 24, 16), (24, 16, 8), (40, 16, 8))


def torus_gather(buf, pieces, coords, device_at, send_sem, recv_sem, near=None, middle=None):
    descs = []
    plus = lambda c, d: lax.rem(c + d + SIDE, SIDE)

    def view(p, where, part):
        start, size, first = pieces[p]
        lo, n = {0: (start, size), 1: (start, first), 2: (start + first, size - first)}[part]
        return buf.at[where[0], where[1], where[2], pl.ds(lo, n), :]

    def copy(p, where, part, axis, step, slot):
        to = list(coords)
        to[axis] = plus(to[axis], step)
        ref = view(p, where, part)
        return pltpu.make_async_remote_copy(
            src_ref=ref, dst_ref=ref, send_sem=send_sem.at[p, slot], recv_sem=recv_sem.at[p, slot],
            device_id={'data': device_at(to)}, device_id_type=pl.DeviceIdType.MESH)

    def send(p, where, part, axis, step, slot):
        c = copy(p, where, part, axis, step, slot)
        c.start()
        descs.append(c)

    def wait(p, where, part, axis, step, slot):
        copy(p, where, part, axis, step, slot).wait_recv()

    orders = [(p, (p + 1) % 3, (p + 2) % 3) for p in range(3)]
    OFFS = (0, -1, 1, 2)

    def at(p, off0, off1, off2):
        where = [None, None, None]
        for axis, off in zip(orders[p], (off0, off1, off2)):
            where[axis] = slice(None) if off is None else (coords[axis] if off == 0 else plus(coords[axis], off))
        return where

    def start_full(p, ph, own, base):
        axis = orders[p][ph]
        send(p, own, 0, axis, 1, base)
        send(p, own, 0, axis, -1, base + 1)

    def relay(p, ph, low, high, base):
        axis = orders[p][ph]
        wait(p, low, 0, axis, 1, base)
        send(p, low, 1, axis, 1, base + 2)
        wait(p, high, 0, axis, 1, base + 1)
        send(p, high, 2, axis, -1, base + 3)

    def finish(p, ph, far, base):
        axis = orders[p][ph]
        wait(p, far, 1, axis, 1, base + 2)
        wait(p, far, 2, axis, 1, base + 3)

    B1, B2, B3 = 0, 4, 20
    for p in range(3):
        start_full(p, 0, at(p, 0, 0, 0), B1)
    for p in range(3):
        start_full(p, 1, at(p, 0, 0, 0), B2)
    for p in range(3):
        relay(p, 0, at(p, -1, 0, 0), at(p, 1, 0, 0), B1)
        start_full(p, 1, at(p, -1, 0, 0), B2 + 4)
        start_full(p, 1, at(p, 1, 0, 0), B2 + 8)
    for p in range(3):
        finish(p, 0, at(p, 2, 0, 0), B1)
        start_full(p, 1, at(p, 2, 0, 0), B2 + 12)
        start_full(p, 2, at(p, None, 0, 0), B3)
    for q in range(4):
        for p in range(3):
            relay(p, 1, at(p, OFFS[q], -1, 0), at(p, OFFS[q], 1, 0), B2 + 4 * q)
    for p in range(3):
        start_full(p, 2, at(p, None, -1, 0), B3 + 4)
        start_full(p, 2, at(p, None, 1, 0), B3 + 8)
    for q in range(4):
        for p in range(3):
            finish(p, 1, at(p, OFFS[q], 2, 0), B2 + 4 * q)
    for p in range(3):
        start_full(p, 2, at(p, None, 2, 0), B3 + 12)
    for q in range(4):
        for p in range(3):
            relay(p, 2, at(p, None, OFFS[q], -1), at(p, None, OFFS[q], 1), B3 + 4 * q)
    if near is not None:
        near()
    for q in range(4):
        if q == 3 and middle is not None:
            middle()
        for p in range(3):
            finish(p, 2, at(p, None, OFFS[q], 2), B3 + 4 * q)
    return descs


def block_index(b):
    return b // (SIDE * SIDE), (b // SIDE) % SIDE, b % SIDE


def place():
    me = lax.axis_index('data')
    core = me % 2
    chip = me // 2
    coords = (chip // (SIDE * SIDE), (chip // SIDE) % SIDE, chip % SIDE)

    def device_at(c):
        return ((c[0] * SIDE + c[1]) * SIDE + c[2]) * 2 + core

    return core, chip, coords, me + 1 - 2 * core, device_at


def greet(devices):
    barrier = pltpu.get_barrier_semaphore()
    for device in devices:
        pl.semaphore_signal(barrier, inc=1, device_id={'data': device}, device_id_type=pl.DeviceIdType.MESH)
    return lambda: pl.semaphore_wait(barrier, len(devices))


def torus_neighbours(coords, device_at):
    found = []
    for axis in range(3):
        for step in (1, -1):
            to = list(coords)
            to[axis] = lax.rem(to[axis] + step + SIDE, SIDE)
            found.append(device_at(to))
    return found


def grids():
    lane = lax.broadcasted_iota(jnp.int32, (HID, LANES), 1)
    sub = lax.broadcasted_iota(jnp.int32, (HID, LANES), 0)
    return lane, sub


def collect_rows(feat_ref, lab_ref, w_ref, wo_ref, m_ref, mo_ref, x_all, xt_all, y_all, pos_ref, vel_ref,
                 x_in, w_tmp, x_send, x_recv, own_sem):
    num_feat = feat_ref.shape[1]
    hidden = w_ref.shape[0]
    core, chip, coords, partner, device_at = place()
    loads = [pltpu.make_async_copy(feat_ref, x_in, own_sem.at[0])]
    eight = pl.multiple_of((chip // 8) * 8, 8)
    for n, ref in enumerate((w_ref, m_ref)):
        loads.append(pltpu.make_async_copy(ref.at[:, pl.ds(eight, 8), :], w_tmp.at[n], own_sem.at[n + 1]))
    for load in loads:
        load.start()
    ready = greet(torus_neighbours(coords, device_at))
    labels = lab_ref[...].astype(jnp.float32)
    loads[0].wait()
    for k in range(8):
        column = jnp.broadcast_to(labels[k:k + 1, :], (LANES, LANES)).T
        spare = lax.broadcasted_iota(jnp.int32, (LANES, LANES), 1)
        rows = pl.ds(k * LANES, LANES)
        x_all[coords[0], coords[1], coords[2], rows, :] = jnp.where(spare == LAB, column, 0.0).astype(jnp.bfloat16)
        x_all[coords[0], coords[1], coords[2], rows, :num_feat] = x_in[rows, :]
    ready()

    def turn(where):
        z, y, x = where
        b = (z * SIDE + y) * SIDE + x
        for k in range(8):
            xt = x_all[z, y, x, k * LANES:(k + 1) * LANES, :].T
            xt_all[b, k] = xt
            y_all[b, k:k + 1, :] = xt[112:128, :].astype(jnp.float32)[LAB - 112:LAB - 111, :]

    def moved(offsets):
        return tuple(lax.rem(c + o, SIDE) for c, o in zip(coords, offsets))

    def three(i):
        return 3 + i

    def near():
        def body(i, carry):
            turn(moved((three(i // 9), three((i // 3) % 3), three(i % 3))))
            return carry
        lax.fori_loop(0, 27, body, 0)

    def middle():
        def body(i, carry):
            u, v = three(i // 3), three(i % 3)
            turn(moved((2, u, v)))
            turn(moved((u, 2, v)))
            turn(moved((u, v, 2)))
            return carry
        lax.fori_loop(0, 9, body, 0)

    def far():
        def body(i, carry):
            u = three(i)
            turn(moved((2, 2, u)))
            turn(moved((2, u, 2)))
            turn(moved((u, 2, 2)))
            return carry
        lax.fori_loop(0, 3, body, 0)
        turn(moved((2, 2, 2)))

    x_descs = torus_gather(x_all, ROW_PIECES, coords, device_at, x_send, x_recv, near, middle)
    far()
    for d in x_descs:
        d.wait_send()
    pos_ref[...] = jnp.zeros_like(pos_ref)
    vel_ref[...] = jnp.zeros_like(vel_ref)
    chain_row = lax.broadcasted_iota(jnp.int32, (hidden, 8, num_feat), 1) == chip % 8
    chain_lane = lax.broadcasted_iota(jnp.int32, wo_ref.shape, 1) == chip
    for n, (ref, last) in enumerate(((pos_ref, wo_ref), (vel_ref, mo_ref))):
        loads[n + 1].wait()
        ref[:hidden, :num_feat] = jnp.sum(jnp.where(chain_row, w_tmp[n], 0.0), axis=1)
        ref[:hidden, OUT:OUT + 1] = jnp.sum(jnp.where(chain_lane, last[...], 0.0), axis=1, keepdims=True)


def gradient(with_loss, *refs):
    def with_acc(pre, grad):
        gradient_body(with_loss, pre, grad, *refs)

    def spec(q):
        return pltpu.ACC(q)((2 * HID, 2 * LANES), jnp.float32)

    pl.run_scoped(with_acc, ((spec(0), spec(1)), (spec(0), spec(1))), (spec(0), spec(1)))


def gradient_body(with_loss, pre_acc, grad_acc, x_all, xt_all, y_all, pos_ref, part_ref, z_all, w2_ref, wbd_ref, b_ref):
    lane, sub = grids()
    def push_forward(b):
        for q in range(2):
            tiles = [jnp.concatenate([xt_all[b, 4 * s + 2 * q], xt_all[b, 4 * s + 2 * q + 1]], axis=1) for s in range(2)]
            pltpu.matmul_push_rhs(jnp.concatenate(tiles, axis=0), staging_register=0, mxu_index=q)

    def forward(u):
        wbd = jnp.concatenate([wbd_ref[0], wbd_ref[1]], axis=1)
        for q in range(2):
            pltpu.matmul_acc_lhs(pre_acc[u][q], wbd, load_staged_rhs=0)

    def rows_to_back(b, u, acc):
        w2 = w2_ref[...].reshape(HID // 8, 8, LANES)
        for q in range(2):
            act = jnp.tanh(pltpu.matmul_pop(pre_acc[u][q]))
            for h in range(2):
                j = 2 * q + h
                parts = []
                for s in range(2):
                    k = 4 * s + j
                    part = act[s * HID:(s + 1) * HID, h * LANES:(h + 1) * LANES].reshape(HID // 8, 8, LANES)
                    z = jnp.sum(part * w2, axis=0)
                    for shift in (4, 2, 1):
                        z = z + pltpu.roll(z, shift, 0)
                    z_all[b, k:k + 1, :] = z[:1]
                    res = jnp.broadcast_to(y_all[b, k:k + 1, :], (8, LANES)) - 1.0 / (1.0 + jnp.exp(-z))
                    weighed = part * res
                    acc = acc + weighed
                    parts.append(((res - weighed * part) * w2).reshape(HID, LANES))
                b_ref[u, j] = jnp.concatenate(parts, axis=0).astype(jnp.bfloat16)
        return acc

    def push_grad(b):
        z, y, x = block_index(b)
        rows = x_all.at[z, y, x]
        for q in range(2):
            tile = jnp.concatenate([rows[256 * q:256 * q + 256, :], rows[512 + 256 * q:768 + 256 * q, :]], axis=1)
            pltpu.matmul_push_rhs(tile, staging_register=1, mxu_index=q)

    def weight_grad(u):
        for q in range(2):
            lhs = jnp.concatenate([b_ref[u, 2 * q], b_ref[u, 2 * q + 1]], axis=1)
            pltpu.matmul_acc_lhs(grad_acc[q], lhs, load_staged_rhs=1)

    pos = pos_ref[...]
    w_in = jnp.where(lane < LAB, pos, 0.0)
    nil = jnp.zeros_like(w_in)
    wbd_ref[0] = jnp.concatenate([w_in, nil], axis=0).astype(jnp.bfloat16)
    wbd_ref[1] = jnp.concatenate([nil, w_in], axis=0).astype(jnp.bfloat16)
    w2_ref[...] = jnp.broadcast_to(pos[:, OUT:OUT + 1], (HID, LANES))
    b_ref[1] = jnp.zeros((4, 2 * HID, LANES), jnp.bfloat16)
    for u in range(2):
        push_forward(u)
        forward(u)
    push_forward(2)
    push_grad(0)

    def pair(i, acc):
        for v in range(UNROLL):
            u = v % 2
            n = UNROLL * i + v
            acc = rows_to_back(n, u, acc)
            forward(u)
            push_forward(jnp.minimum(n + 3, BLOCKS - 1))
            weight_grad(1 - u)
            push_grad(n)
        return acc

    acc = lax.fori_loop(0, BLOCKS // UNROLL, pair, jnp.zeros((HID // 8, 8, LANES), jnp.float32)).reshape(HID, LANES)
    weight_grad(1)
    for u in range(2):
        if u == 0:
            forward(u)
        for q in range(2):
            pltpu.matmul_pop(pre_acc[u][q])
    whole = pltpu.matmul_pop(grad_acc[0]) + pltpu.matmul_pop(grad_acc[1])
    grad = whole[:HID, :LANES] + whole[HID:, LANES:]
    grad = jnp.where(lane < LAB, grad, jnp.where(lane == OUT, jnp.sum(acc, axis=1, keepdims=True), 0.0))
    if with_loss:
        def loss_block(b, total):
            z = z_all[b]
            return total + (jnp.maximum(z, 0.0) + jnp.log1p(jnp.exp(-jnp.abs(z))) - y_all[b] * z)

        total = lax.fori_loop(0, BLOCKS, loss_block, jnp.zeros((8, LANES), jnp.float32))
        total = jnp.sum(jnp.sum(total, axis=1, keepdims=True), axis=0, keepdims=True)
        grad = jnp.where((lane == LOSS) & (sub == 0), total, grad)
    part_ref[...] = grad


def both_parts(part_ref, rcv, partner, e_send, e_recv):
    ex = pltpu.make_async_remote_copy(
        src_ref=part_ref, dst_ref=rcv, send_sem=e_send, recv_sem=e_recv,
        device_id={'data': partner}, device_id_type=pl.DeviceIdType.MESH)
    ex.start()
    ex.wait()
    return part_ref[...] + rcv[...]


def kick(vel, pos, total, rate):
    lane, _ = grids()
    is_param = (lane < LAB) | (lane == OUT)
    return vel + rate * jnp.where(is_param, total - pos * (1.0 / PRIOR_VAR), 0.0)


def leap(rate, step_size, part_ref, pos_ref, vel_ref, pos_new, vel_new, rcv, e_send, e_recv):
    _, _, _, partner, _ = place()
    greet([partner])()
    total = both_parts(part_ref, rcv, partner, e_send, e_recv)
    vel = kick(vel_ref[...], pos_ref[...], total, rate)
    vel_new[...] = vel
    pos_new[...] = pos_ref[...] + step_size * vel


def finish(rate, hidden, part_ref, pos_ref, vel_ref, all_ref, rcv, e_send, e_recv, o_send, o_recv, s_send, s_recv):
    core, _, coords, partner, device_at = place()
    greet(torus_neighbours(coords, device_at) + [partner])()
    total = both_parts(part_ref, rcv, partner, e_send, e_recv)
    lane, sub = grids()
    pos = pos_ref[...]
    vel = kick(vel_ref[...], pos, total, rate)
    loss = total[:1, LOSS:LOSS + 1]
    square = (pos * pos) * (1.0 / (2.0 * PRIOR_VAR)) + 0.5 * (vel * vel)
    energy = loss + jnp.sum(jnp.sum(square, axis=1, keepdims=True), axis=0, keepdims=True)
    tails = []
    for value in (pos, vel):
        w2 = jnp.broadcast_to(value[:, OUT:OUT + 1], (HID, LANES))
        row = jnp.concatenate([w2, jnp.zeros((LANES - HID, LANES), jnp.float32)], axis=0).T[:1, :]
        tails.append(jnp.broadcast_to(row, (HID, LANES)))
    tails[0] = jnp.where(lane == hidden, energy, tails[0])
    outs = [jnp.where(sub == hidden, t, v) for t, v in zip(tails, (pos, vel))]
    all_ref[core, coords[0], coords[1], coords[2]] = jnp.where(core == 0, outs[0], outs[1])
    o_descs = torus_gather(all_ref.at[core], OUT_PIECES, coords, device_at, o_send, o_recv)
    swap = pltpu.make_async_remote_copy(
        src_ref=all_ref.at[core], dst_ref=all_ref.at[core], send_sem=s_send, recv_sem=s_recv,
        device_id={'data': partner}, device_id_type=pl.DeviceIdType.MESH)
    swap.start()
    for d in o_descs:
        d.wait_send()
    swap.wait_send()
    pltpu.make_async_remote_copy(
        src_ref=all_ref.at[1 - core], dst_ref=all_ref.at[1 - core], send_sem=s_send, recv_sem=s_recv,
        device_id={'data': partner}, device_id_type=pl.DeviceIdType.MESH).wait_recv()


def spread_out(flat, w_end, wo_end, m_end, mo_end, e_end):
    hidden, _, num_feat = w_end.shape

    def spread(h, carry):
        for n, ref in enumerate((w_end, m_end)):
            for c in range(0, BLOCKS, 8):
                ref[h, c:c + 8, :] = flat[n, pl.ds(c * HID + h, 8, stride=HID), :][:, :num_feat]
        return carry

    lax.fori_loop(0, hidden, spread, 0)
    for n, ref in enumerate((wo_end, mo_end)):
        tail = jnp.concatenate([flat[n, pl.ds(c * HID + hidden, 8, stride=HID), :] for c in range(0, BLOCKS, 8)]
                               + [jnp.zeros((LANES - BLOCKS, LANES), jnp.float32)], axis=0).T
        ref[...] = tail[:hidden, :BLOCKS]
        if n == 0:
            e_end[...] = tail[hidden:hidden + 1, :BLOCKS]


VMEM = pl.BlockSpec(memory_space=pltpu.VMEM)
HBM = pl.BlockSpec(memory_space=pltpu.HBM)
DMA = pltpu.SemaphoreType.DMA


def struct(shape, dtype=jnp.float32):
    return jax.ShapeDtypeStruct(shape, dtype)


def call(kernel, name, inputs, outs, scratch, mib, collective=None, in_specs=None):
    extra = {} if collective is None else dict(collective_id=collective, has_side_effects=True)
    return pl.pallas_call(
        kernel, out_shape=outs, in_specs=in_specs or [VMEM] * len(inputs),
        out_specs=[VMEM] * len(outs) if isinstance(outs, list) else VMEM, scratch_shapes=scratch,
        compiler_params=pltpu.CompilerParams(vmem_limit_bytes=mib * MIB, **extra), name=name)(*inputs)


def grad_call(data, pos, with_loss):
    bf16 = jnp.bfloat16
    return call(functools.partial(gradient, with_loss), 'gradient', (*data, pos), struct((HID, LANES)), [
        pltpu.VMEM((BLOCKS, 8, LANES), jnp.float32),
        pltpu.VMEM((HID, LANES), jnp.float32),
        pltpu.VMEM((2, 2 * HID, LANES), bf16),
        pltpu.VMEM((2, 4, 2 * HID, LANES), bf16)], 4)


def run_all(feats, labels, w_in, w_out, mom_in, mom_out, step_size):
    rows, num_feat = feats.shape
    hidden, chains, _ = w_in.shape
    f32, bf16 = jnp.float32, jnp.bfloat16
    state = struct((HID, LANES))
    outs = [struct((SIDE, SIDE, SIDE, rows, LANES), bf16), struct((BLOCKS, rows // LANES, LANES, LANES), bf16), struct((BLOCKS, 8, LANES)), state, state]
    *data, pos, vel = call(
        collect_rows, 'collect', (feats, labels, w_in, w_out, mom_in, mom_out), outs,
        [pltpu.VMEM((rows, num_feat), bf16), pltpu.VMEM((2, hidden, 8, num_feat), f32), DMA((3, 36)), DMA((3, 36)), DMA((3,))],
        4, 0, [HBM, VMEM, HBM, VMEM, HBM, VMEM])
    for k in range(LEAPS):
        part = grad_call(data, pos, False)
        rate = 0.5 * step_size if k == 0 else step_size
        pos, vel = call(functools.partial(leap, rate, step_size), 'leap', (part, pos, vel), [state, state],
                        [pltpu.VMEM((HID, LANES), f32), DMA, DMA], 1, 1 if k == 0 else 2)
    part = grad_call(data, pos, True)
    every = call(functools.partial(finish, 0.5 * step_size, hidden), 'finish', (part, pos, vel), struct((2, SIDE, SIDE, SIDE, HID, LANES)),
                 [pltpu.VMEM((HID, LANES), f32), DMA, DMA, DMA((3, 36)), DMA((3, 36)), DMA, DMA], 2, 3)
    ends = [struct(w_in.shape), struct(w_out.shape)] * 2 + [struct((1, chains))]
    return call(spread_out, 'spread', (every.reshape(2, BLOCKS * HID, LANES),), ends, [], 8)


def solution(mesh):
    row_spec = P('data', None)
    label_spec = P('data')
    in_spec = P(None, 'parts', None)
    out_spec = P('parts', None)
    chain_spec = P('parts')

    def run_chains(feats, labels, w_in, w_out, mom_in, mom_out):
        num_rows, num_feat = feats.shape
        hidden = w_in.shape[2]
        step_size = 1.0 / math.sqrt(num_rows * (num_feat + hidden))

        def device_body(x_rows, y_rows, pos_in, pos_out, vel_in, vel_out):
            turned = [jnp.transpose(v) for v in (pos_in, pos_out, vel_in, vel_out)]
            ends = run_all(x_rows, y_rows.reshape(8, LANES), *turned, step_size)
            return tuple(jnp.transpose(v) for v in ends[:4]) + (ends[4].reshape(-1),)

        mapped = jax.shard_map(device_body, mesh=mesh, in_specs=(row_spec, label_spec, in_spec, out_spec, in_spec, out_spec), out_specs=(in_spec, out_spec, in_spec, out_spec, chain_spec), check_vma=False)
        return mapped(feats, labels, w_in, w_out, mom_in, mom_out)

    return run_chains
```

time: 282 us -> 273 us (0.968)
  Pallas kernels: 275 us -> 265 us
    pallas_call x1 -> x36, Pallas kernels: 275 us -> 265 us  [call(): pl.pallas_call(kernel, out_shape=outs, in_specs=in_specs or [VMEM] * len(...]
    unnamed x13 -> x12, local copies, waits for them, and re-layouts: 5.82 us -> 5.98 us
where the time goes in v3:
time: 273 us; the launch traced here: 272 us
  Pallas kernels  265 us (97%)
  local copies, waits for them, and re-layouts  5.98 us (2%)
    pallas_call x36, Pallas kernels, call(): pl.pallas_call(kernel, out_shape=outs, in_specs=in_specs or [VMEM] * len(...  265 us
    unnamed x12, local copies, waits for them, and re-layouts  5.98 us

profile of v3, /device:TPU:1, one launch (start us, length us, event | category | flops | bytes accessed | tf_op | source)
XLA Modules:
  0.0 272.4 jit_solution(6218027830666330439)
XLA Ops:
  0.6 1.4 copy-done
  2.1 1.4 copy-done.1
  6.6 71.2 %collect.1 = (bf16[4,4,4,1024,128]{4,3,2,1,0:T(8,128)(2,1)S(1)}, bf16[64,8,128,128]{3,2,1,0:T(8,128)(2,1)S(1)}, f32[64,8,128]{2,1,0:T(8,128)S(1)}, f32[56,128]{1,0:T(8,128)S(1)}, f32[56,128]{1,0:T(8,128)S(1)}) custom-call(bf16[1024,123]{1,0:T(8,128)(2,1)S(1)} %copy-done.2, s32[8,128]{1,0:T(8,128)S(1)} %bitcast.16, f32[50,64,123]{2,1,0:T(8,128)S(1)} %bitcast.12, ...), custom_call_target="tpu_custom_call" | custom-call | tf_op jit(solution)/shard_map/collect/pallas_call | solution.py:412
  77.8 8.1 %gradient.17.part_ref = f32[56,128]{1,0:T(8,128)S(1)} custom-call(bf16[4,4,4,1024,128]{4,3,2,1,0:T(8,128)(2,1)S(1)} %get-tuple-element.47.refs_0_, bf16[64,8,128,128]{3,2,1,0:T(8,128)(2,1)S(1)} %get-tuple-element.48.refs_1_, f32[64,8,128]{2,1,0:T(8,128)S(1)} %get-tuple-element.49.refs_2_, f32[56,128]{1,0:T(8,128)S(1)} %get-tuple-element.50.refs_3_.pos_ref), custom_call_target="tpu_custom_call" | custom-call | tf_op jit(solution)/shard_map/gradient/pallas_call | solution.py:412
  86.0 4.2 %leap.16 = (f32[56,128]{1,0:T(8,128)S(1)}, f32[56,128]{1,0:T(8,128)S(1)}) custom-call(f32[56,128]{1,0:T(8,128)S(1)} %gradient.17.part_ref, f32[56,128]{1,0:T(8,128)S(1)} %get-tuple-element.50.refs_3_.pos_ref, f32[56,128]{1,0:T(8,128)S(1)} %get-tuple-element.51.vel_ref), custom_call_target="tpu_custom_call" | custom-call | tf_op jit(solution)/shard_map/leap/pallas_call | solution.py:412
  90.2 8.1 %gradient.18.part_ref = f32[56,128]{1,0:T(8,128)S(1)} custom-call(bf16[4,4,4,1024,128]{4,3,2,1,0:T(8,128)(2,1)S(1)} %get-tuple-element.47.refs_0_, bf16[64,8,128,128]{3,2,1,0:T(8,128)(2,1)S(1)} %get-tuple-element.48.refs_1_, f32[64,8,128]{2,1,0:T(8,128)S(1)} %get-tuple-element.49.refs_2_, f32[56,128]{1,0:T(8,128)S(1)} %get-tuple-element.52.refs_3_.pos_ref), custom_call_target="tpu_custom_call" | custom-call | tf_op jit(solution)/shard_map/gradient/pallas_call | solution.py:412
  98.3 1.2 leap.17
  99.6 8.1 %gradient.19.part_ref = f32[56,128]{1,0:T(8,128)S(1)} custom-call(bf16[4,4,4,1024,128]{4,3,2,1,0:T(8,128)(2,1)S(1)} %get-tuple-element.47.refs_0_, bf16[64,8,128,128]{3,2,1,0:T(8,128)(2,1)S(1)} %get-tuple-element.48.refs_1_, f32[64,8,128]{2,1,0:T(8,128)S(1)} %get-tuple-element.49.refs_2_, f32[56,128]{1,0:T(8,128)S(1)} %get-tuple-element.54.refs_3_.pos_ref), custom_call_target="tpu_custom_call" | custom-call | tf_op jit(solution)/shard_map/gradient/pallas_call | solution.py:412
  107.7 1.3 leap.18
  109.0 8.1 %gradient.20.part_ref = f32[56,128]{1,0:T(8,128)S(1)} custom-call(bf16[4,4,4,1024,128]{4,3,2,1,0:T(8,128)(2,1)S(1)} %get-tuple-element.47.refs_0_, bf16[64,8,128,128]{3,2,1,0:T(8,128)(2,1)S(1)} %get-tuple-element.48.refs_1_, f32[64,8,128]{2,1,0:T(8,128)S(1)} %get-tuple-element.49.refs_2_, f32[56,128]{1,0:T(8,128)S(1)} %get-tuple-element.56.refs_3_.pos_ref), custom_call_target="tpu_custom_call" | custom-call | tf_op jit(solution)/shard_map/gradient/pallas_call | solution.py:412
  117.1 1.2 leap.19
  118.4 8.1 %gradient.21.part_ref = f32[56,128]{1,0:T(8,128)S(1)} custom-call(bf16[4,4,4,1024,128]{4,3,2,1,0:T(8,128)(2,1)S(1)} %get-tuple-element.47.refs_0_, bf16[64,8,128,128]{3,2,1,0:T(8,128)(2,1)S(1)} %get-tuple-element.48.refs_1_, f32[64,8,128]{2,1,0:T(8,128)S(1)} %get-tuple-element.49.refs_2_, f32[56,128]{1,0:T(8,128)S(1)} %get-tuple-element.58.refs_3_.pos_ref), custom_call_target="tpu_custom_call" | custom-call | tf_op jit(solution)/shard_map/gradient/pallas_call | solution.py:412
  126.5 1.3 leap.20
  127.8 8.1 %gradient.22.part_ref = f32[56,128]{1,0:T(8,128)S(1)} custom-call(bf16[4,4,4,1024,128]{4,3,2,1,0:T(8,128)(2,1)S(1)} %get-tuple-element.47.refs_0_, bf16[64,8,128,128]{3,2,1,0:T(8,128)(2,1)S(1)} %get-tuple-element.48.refs_1_, f32[64,8,128]{2,1,0:T(8,128)S(1)} %get-tuple-element.49.refs_2_, f32[56,128]{1,0:T(8,128)S(1)} %get-tuple-element.60.refs_3_.pos_ref), custom_call_target="tpu_custom_call" | custom-call | tf_op jit(solution)/shard_map/gradient/pallas_call | solution.py:412
  137.2 8.1 %gradient.23.part_ref = f32[56,128]{1,0:T(8,128)S(1)} custom-call(bf16[4,4,4,1024,128]{4,3,2,1,0:T(8,128)(2,1)S(1)} %get-tuple-element.47.refs_0_, bf16[64,8,128,128]{3,2,1,0:T(8,128)(2,1)S(1)} %get-tuple-element.48.refs_1_, f32[64,8,128]{2,1,0:T(8,128)S(1)} %get-tuple-element.49.refs_2_, f32[56,128]{1,0:T(8,128)S(1)} %get-tuple-element.62.refs_3_.pos_ref), custom_call_target="tpu_custom_call" | custom-call | tf_op jit(solution)/shard_map/gradient/pallas_call | solution.py:412
  145.3 1.3 leap.22
  146.6 8.1 %gradient.24.part_ref = f32[56,128]{1,0:T(8,128)S(1)} custom-call(bf16[4,4,4,1024,128]{4,3,2,1,0:T(8,128)(2,1)S(1)} %get-tuple-element.47.refs_0_, bf16[64,8,128,128]{3,2,1,0:T(8,128)(2,1)S(1)} %get-tuple-element.48.refs_1_, f32[64,8,128]{2,1,0:T(8,128)S(1)} %get-tuple-element.49.refs_2_, f32[56,128]{1,0:T(8,128)S(1)} %get-tuple-element.64.refs_3_.pos_ref), custom_call_target="tpu_custom_call" | custom-call | tf_op jit(solution)/shard_map/gradient/pallas_call | solution.py:412
  156.0 8.1 %gradient.25.part_ref = f32[56,128]{1,0:T(8,128)S(1)} custom-call(bf16[4,4,4,1024,128]{4,3,2,1,0:T(8,128)(2,1)S(1)} %get-tuple-element.47.refs_0_, bf16[64,8,128,128]{3,2,1,0:T(8,128)(2,1)S(1)} %get-tuple-element.48.refs_1_, f32[64,8,128]{2,1,0:T(8,128)S(1)} %get-tuple-element.49.refs_2_, f32[56,128]{1,0:T(8,128)S(1)} %get-tuple-element.66.refs_3_.pos_ref), custom_call_target="tpu_custom_call" | custom-call | tf_op jit(solution)/shard_map/gradient/pallas_call | solution.py:412
  164.2 1.3 leap.24
  165.4 8.1 %gradient.26.part_ref = f32[56,128]{1,0:T(8,128)S(1)} custom-call(bf16[4,4,4,1024,128]{4,3,2,1,0:T(8,128)(2,1)S(1)} %get-tuple-element.47.refs_0_, bf16[64,8,128,128]{3,2,1,0:T(8,128)(2,1)S(1)} %get-tuple-element.48.refs_1_, f32[64,8,128]{2,1,0:T(8,128)S(1)} %get-tuple-element.49.refs_2_, f32[56,128]{1,0:T(8,128)S(1)} %get-tuple-element.68.refs_3_.pos_ref), custom_call_target="tpu_custom_call" | custom-call | tf_op jit(solution)/shard_map/gradient/pallas_call | solution.py:412
  174.8 8.1 %gradient.27.part_ref = f32[56,128]{1,0:T(8,128)S(1)} custom-call(bf16[4,4,4,1024,128]{4,3,2,1,0:T(8,128)(2,1)S(1)} %get-tuple-element.47.refs_0_, bf16[64,8,128,128]{3,2,1,0:T(8,128)(2,1)S(1)} %get-tuple-element.48.refs_1_, f32[64,8,128]{2,1,0:T(8,128)S(1)} %get-tuple-element.49.refs_2_, f32[56,128]{1,0:T(8,128)S(1)} %get-tuple-element.70.refs_3_.pos_ref), custom_call_target="tpu_custom_call" | custom-call | tf_op jit(solution)/shard_map/gradient/pallas_call | solution.py:412
  183.0 1.3 leap.26
  184.2 8.1 %gradient.28.part_ref = f32[56,128]{1,0:T(8,128)S(1)} custom-call(bf16[4,4,4,1024,128]{4,3,2,1,0:T(8,128)(2,1)S(1)} %get-tuple-element.47.refs_0_, bf16[64,8,128,128]{3,2,1,0:T(8,128)(2,1)S(1)} %get-tuple-element.48.refs_1_, f32[64,8,128]{2,1,0:T(8,128)S(1)} %get-tuple-element.49.refs_2_, f32[56,128]{1,0:T(8,128)S(1)} %get-tuple-element.72.refs_3_.pos_ref), custom_call_target="tpu_custom_call" | custom-call | tf_op jit(solution)/shard_map/gradient/pallas_call | solution.py:412
  193.6 8.1 %gradient.29.part_ref = f32[56,128]{1,0:T(8,128)S(1)} custom-call(bf16[4,4,4,1024,128]{4,3,2,1,0:T(8,128)(2,1)S(1)} %get-tuple-element.47.refs_0_, bf16[64,8,128,128]{3,2,1,0:T(8,128)(2,1)S(1)} %get-tuple-element.48.refs_1_, f32[64,8,128]{2,1,0:T(8,128)S(1)} %get-tuple-element.49.refs_2_, f32[56,128]{1,0:T(8,128)S(1)} %get-tuple-element.74.refs_3_.pos_ref), custom_call_target="tpu_custom_call" | custom-call | tf_op jit(solution)/shard_map/gradient/pallas_call | solution.py:412
  201.8 1.3 leap.28
  203.0 8.1 %gradient.30.part_ref = f32[56,128]{1,0:T(8,128)S(1)} custom-call(bf16[4,4,4,1024,128]{4,3,2,1,0:T(8,128)(2,1)S(1)} %get-tuple-element.47.refs_0_, bf16[64,8,128,128]{3,2,1,0:T(8,128)(2,1)S(1)} %get-tuple-element.48.refs_1_, f32[64,8,128]{2,1,0:T(8,128)S(1)} %get-tuple-element.49.refs_2_, f32[56,128]{1,0:T(8,128)S(1)} %get-tuple-element.76.refs_3_.pos_ref), custom_call_target="tpu_custom_call" | custom-call | tf_op jit(solution)/shard_map/gradient/pallas_call | solution.py:412
  212.4 8.3 %gradient.31.part_ref = f32[56,128]{1,0:T(8,128)S(1)} custom-call(bf16[4,4,4,1024,128]{4,3,2,1,0:T(8,128)(2,1)S(1)} %get-tuple-element.47.refs_0_, bf16[64,8,128,128]{3,2,1,0:T(8,128)(2,1)S(1)} %get-tuple-element.48.refs_1_, f32[64,8,128]{2,1,0:T(8,128)S(1)} %get-tuple-element.49.refs_2_, f32[56,128]{1,0:T(8,128)S(1)} %get-tuple-element.78.refs_3_.pos_ref), custom_call_target="tpu_custom_call" | custom-call | tf_op jit(solution)/shard_map/gradient/pallas_call | solution.py:412
  220.7 1.3 leap.30
  222.0 8.1 %gradient.32.part_ref = f32[56,128]{1,0:T(8,128)S(1)} custom-call(bf16[4,4,4,1024,128]{4,3,2,1,0:T(8,128)(2,1)S(1)} %get-tuple-element.47.refs_0_, bf16[64,8,128,128]{3,2,1,0:T(8,128)(2,1)S(1)} %get-tuple-element.48.refs_1_, f32[64,8,128]{2,1,0:T(8,128)S(1)} %get-tuple-element.49.refs_2_, f32[56,128]{1,0:T(8,128)S(1)} %get-tuple-element.80.refs_3_.pos_ref), custom_call_target="tpu_custom_call" | custom-call | tf_op jit(solution)/shard_map/gradient/pallas_call | solution.py:412
  231.4 9.6 %gradient.33.part_ref = f32[56,128]{1,0:T(8,128)S(1)} custom-call(bf16[4,4,4,1024,128]{4,3,2,1,0:T(8,128)(2,1)S(1)} %get-tuple-element.47.refs_0_, bf16[64,8,128,128]{3,2,1,0:T(8,128)(2,1)S(1)} %get-tuple-element.48.refs_1_, f32[64,8,128]{2,1,0:T(8,128)S(1)} %get-tuple-element.49.refs_2_, f32[56,128]{1,0:T(8,128)S(1)} %get-tuple-element.82.refs_3_.pos_ref), custom_call_target="tpu_custom_call" | custom-call | tf_op jit(solution)/shard_map/gradient/pallas_call | solution.py:412
  241.0 28.7 %finish.1 = f32[2,4,4,4,56,128]{5,4,3,2,1,0:T(8,128)S(1)} custom-call(f32[56,128]{1,0:T(8,128)S(1)} %gradient.33.part_ref, f32[56,128]{1,0:T(8,128)S(1)} %get-tuple-element.82.refs_3_.pos_ref, f32[56,128]{1,0:T(8,128)S(1)} %get-tuple-element.83.vel_ref), custom_call_target="tpu_custom_call" | custom-call | tf_op jit(solution)/shard_map/finish/pallas_call | solution.py:412
  269.7 2.7 spread.1
  (16 shorter events, 10.6 us)
Async XLA Ops:
  0.6 1.4 copy-start
  2.1 1.4 copy-start.1
  3.5 0.9 copy-start.2
  4.4 0.7 copy-start.3
  5.2 0.7 copy-start.4
  5.9 0.7 copy-start.5

commit v4 on v3

--- a/solution.py
+++ b/solution.py
@@ -17,14 +17,16 @@
 LAB = 123
 LOSS = 124
 OUT = 127
-UNROLL = 4
+UNROLL = 8
 MIB = 2 ** 20
-ROW_PIECES = ((0, 352, 176), (352, 336, 176), (688, 336, 176))
+PREPARE_BYTES = 57000000
+ROW_PIECES = ((0, 344, 176), (344, 344, 176), (688, 336, 168))
 OUT_PIECES = ((0, 24, 16), (24, 16, 8), (40, 16, 8))
 
 
-def torus_gather(buf, pieces, coords, device_at, send_sem, recv_sem, near=None, middle=None):
+def torus_gather(buf, pieces, coords, device_at, send_sem, recv_sem, near=None, middle=None, share=None):
     descs = []
+    direct = share is not None
     plus = lambda c, d: lax.rem(c + d + SIDE, SIDE)
 
     def view(p, where, part):
@@ -61,16 +63,24 @@
         axis = orders[p][ph]
         send(p, own, 0, axis, 1, base)
         send(p, own, 0, axis, -1, base + 1)
+        if direct and ph < 2:
+            send(p, own, 0, axis, 2, base + 2)
 
     def relay(p, ph, low, high, base):
         axis = orders[p][ph]
         wait(p, low, 0, axis, 1, base)
+        if direct and ph < 2:
+            wait(p, high, 0, axis, 1, base + 1)
+            return
         send(p, low, 1, axis, 1, base + 2)
         wait(p, high, 0, axis, 1, base + 1)
         send(p, high, 2, axis, -1, base + 3)
 
     def finish(p, ph, far, base):
         axis = orders[p][ph]
+        if direct and ph < 2:
+            wait(p, far, 0, axis, 1, base + 2)
+            return
         wait(p, far, 1, axis, 1, base + 2)
         wait(p, far, 2, axis, 1, base + 3)
 
@@ -103,11 +113,18 @@
             relay(p, 2, at(p, None, OFFS[q], -1), at(p, None, OFFS[q], 1), B3 + 4 * q)
     if near is not None:
         near()
+    if share is not None:
+        for p in range(3):
+            for i in range(3):
+                share(p, i, at(p, None, None, OFFS[i]))
     for q in range(4):
         if q == 3 and middle is not None:
             middle()
         for p in range(3):
             finish(p, 2, at(p, None, OFFS[q], 2), B3 + 4 * q)
+    if share is not None:
+        for p in range(3):
+            share(p, 3, at(p, None, None, 2))
     return descs
 
 
@@ -134,10 +151,10 @@
     return lambda: pl.semaphore_wait(barrier, len(devices))
 
 
-def torus_neighbours(coords, device_at):
+def torus_neighbours(coords, device_at, steps=(1, -1)):
     found = []
     for axis in range(3):
-        for step in (1, -1):
+        for step in steps:
             to = list(coords)
             to[axis] = lax.rem(to[axis] + step + SIDE, SIDE)
             found.append(device_at(to))
@@ -150,26 +167,42 @@
     return lane, sub
 
 
-def collect_rows(feat_ref, lab_ref, w_ref, wo_ref, m_ref, mo_ref, x_all, xt_all, y_all, pos_ref, vel_ref,
-                 x_in, w_tmp, x_send, x_recv, own_sem):
+def prepare(feat_ref, lab_ref, w_ref, wo_ref, m_ref, mo_ref, own_ref, pos_ref, vel_ref, x_in, w_tmp, lab_tmp, o_tmp, sem):
     num_feat = feat_ref.shape[1]
     hidden = w_ref.shape[0]
-    core, chip, coords, partner, device_at = place()
-    loads = [pltpu.make_async_copy(feat_ref, x_in, own_sem.at[0])]
+    chip = lax.axis_index('data') // 2
     eight = pl.multiple_of((chip // 8) * 8, 8)
+    loads = [pltpu.make_async_copy(feat_ref, x_in, sem.at[0]), pltpu.make_async_copy(lab_ref, lab_tmp, sem.at[1])]
     for n, ref in enumerate((w_ref, m_ref)):
-        loads.append(pltpu.make_async_copy(ref.at[:, pl.ds(eight, 8), :], w_tmp.at[n], own_sem.at[n + 1]))
+        loads.append(pltpu.make_async_copy(ref.at[:, pl.ds(eight, 8), :], w_tmp.at[n], sem.at[n + 2]))
+    for n, ref in enumerate((wo_ref, mo_ref)):
+        loads.append(pltpu.make_async_copy(ref, o_tmp.at[n], sem.at[n + 4]))
     for load in loads:
         load.start()
-    ready = greet(torus_neighbours(coords, device_at))
-    labels = lab_ref[...].astype(jnp.float32)
-    loads[0].wait()
+    pos_ref[...] = jnp.zeros_like(pos_ref)
+    vel_ref[...] = jnp.zeros_like(vel_ref)
+    for load in loads:
+        load.wait()
+    labels = lab_tmp[...].astype(jnp.float32)
     for k in range(8):
         column = jnp.broadcast_to(labels[k:k + 1, :], (LANES, LANES)).T
         spare = lax.broadcasted_iota(jnp.int32, (LANES, LANES), 1)
         rows = pl.ds(k * LANES, LANES)
-        x_all[coords[0], coords[1], coords[2], rows, :] = jnp.where(spare == LAB, column, 0.0).astype(jnp.bfloat16)
-        x_all[coords[0], coords[1], coords[2], rows, :num_feat] = x_in[rows, :]
+        own_ref[rows, :] = jnp.where(spare == LAB, column, 0.0).astype(jnp.bfloat16)
+        own_ref[rows, :num_feat] = x_in[rows, :]
+    chain_row = lax.broadcasted_iota(jnp.int32, (hidden, 8, num_feat), 1) == chip % 8
+    chain_lane = lax.broadcasted_iota(jnp.int32, wo_ref.shape, 1) == chip
+    for n, ref in enumerate((pos_ref, vel_ref)):
+        ref[:hidden, :num_feat] = jnp.sum(jnp.where(chain_row, w_tmp[n], 0.0), axis=1)
+        ref[:hidden, OUT:OUT + 1] = jnp.sum(jnp.where(chain_lane, o_tmp[n], 0.0), axis=1, keepdims=True)
+
+
+def collect_rows(own_ref, x_all, xt_all, y_all, x_send, x_recv, own_sem):
+    core, chip, coords, partner, device_at = place()
+    own = pltpu.make_async_copy(own_ref, x_all.at[coords[0], coords[1], coords[2]], own_sem)
+    own.start()
+    ready = greet(torus_neighbours(coords, device_at))
+    own.wait()
     ready()
 
     def turn(where):
@@ -215,14 +248,6 @@
     far()
     for d in x_descs:
         d.wait_send()
-    pos_ref[...] = jnp.zeros_like(pos_ref)
-    vel_ref[...] = jnp.zeros_like(vel_ref)
-    chain_row = lax.broadcasted_iota(jnp.int32, (hidden, 8, num_feat), 1) == chip % 8
-    chain_lane = lax.broadcasted_iota(jnp.int32, wo_ref.shape, 1) == chip
-    for n, (ref, last) in enumerate(((pos_ref, wo_ref), (vel_ref, mo_ref))):
-        loads[n + 1].wait()
-        ref[:hidden, :num_feat] = jnp.sum(jnp.where(chain_row, w_tmp[n], 0.0), axis=1)
-        ref[:hidden, OUT:OUT + 1] = jnp.sum(jnp.where(chain_lane, last[...], 0.0), axis=1, keepdims=True)
 
 
 def gradient(with_loss, *refs):
@@ -260,7 +285,8 @@
                     z = jnp.sum(part * w2, axis=0)
                     for shift in (4, 2, 1):
                         z = z + pltpu.roll(z, shift, 0)
-                    z_all[b, k:k + 1, :] = z[:1]
+                    if with_loss:
+                        z_all[b, k:k + 1, :] = z[:1]
                     res = jnp.broadcast_to(y_all[b, k:k + 1, :], (8, LANES)) - 1.0 / (1.0 + jnp.exp(-z))
                     weighed = part * res
                     acc = acc + weighed
@@ -351,7 +377,7 @@
 
 def finish(rate, hidden, part_ref, pos_ref, vel_ref, all_ref, rcv, e_send, e_recv, o_send, o_recv, s_send, s_recv):
     core, _, coords, partner, device_at = place()
-    greet(torus_neighbours(coords, device_at) + [partner])()
+    greet(torus_neighbours(coords, device_at, (1, -1, 2)) + [partner])()
     total = both_parts(part_ref, rcv, partner, e_send, e_recv)
     lane, sub = grids()
     pos = pos_ref[...]
@@ -367,17 +393,25 @@
     tails[0] = jnp.where(lane == hidden, energy, tails[0])
     outs = [jnp.where(sub == hidden, t, v) for t, v in zip(tails, (pos, vel))]
     all_ref[core, coords[0], coords[1], coords[2]] = jnp.where(core == 0, outs[0], outs[1])
-    o_descs = torus_gather(all_ref.at[core], OUT_PIECES, coords, device_at, o_send, o_recv)
-    swap = pltpu.make_async_remote_copy(
-        src_ref=all_ref.at[core], dst_ref=all_ref.at[core], send_sem=s_send, recv_sem=s_recv,
-        device_id={'data': partner}, device_id_type=pl.DeviceIdType.MESH)
-    swap.start()
+    shared = []
+
+    def across(side, p, i, where):
+        start, size, _ = OUT_PIECES[p]
+        ref = all_ref.at[side, where[0], where[1], where[2], pl.ds(start, size), :]
+        return pltpu.make_async_remote_copy(
+            src_ref=ref, dst_ref=ref, send_sem=s_send.at[p, i], recv_sem=s_recv.at[p, i],
+            device_id={'data': partner}, device_id_type=pl.DeviceIdType.MESH)
+
+    def share(p, i, where):
+        across(core, p, i, where).start()
+        shared.append((p, i, where))
+
+    o_descs = torus_gather(all_ref.at[core], OUT_PIECES, coords, device_at, o_send, o_recv, share=share)
     for d in o_descs:
         d.wait_send()
-    swap.wait_send()
-    pltpu.make_async_remote_copy(
-        src_ref=all_ref.at[1 - core], dst_ref=all_ref.at[1 - core], send_sem=s_send, recv_sem=s_recv,
-        device_id={'data': partner}, device_id_type=pl.DeviceIdType.MESH).wait_recv()
+    for item in shared:
+        across(core, *item).wait_send()
+        across(1 - core, *item).wait_recv()
 
 
 def spread_out(flat, w_end, wo_end, m_end, mo_end, e_end):
@@ -407,12 +441,12 @@
     return jax.ShapeDtypeStruct(shape, dtype)
 
 
-def call(kernel, name, inputs, outs, scratch, mib, collective=None, in_specs=None):
+def call(kernel, name, inputs, outs, scratch, limit, collective=None, in_specs=None):
     extra = {} if collective is None else dict(collective_id=collective, has_side_effects=True)
     return pl.pallas_call(
         kernel, out_shape=outs, in_specs=in_specs or [VMEM] * len(inputs),
         out_specs=[VMEM] * len(outs) if isinstance(outs, list) else VMEM, scratch_shapes=scratch,
-        compiler_params=pltpu.CompilerParams(vmem_limit_bytes=mib * MIB, **extra), name=name)(*inputs)
+        compiler_params=pltpu.CompilerParams(vmem_limit_bytes=limit, **extra), name=name)(*inputs)
 
 
 def grad_call(data, pos, with_loss):
@@ -421,7 +455,7 @@
         pltpu.VMEM((BLOCKS, 8, LANES), jnp.float32),
         pltpu.VMEM((HID, LANES), jnp.float32),
         pltpu.VMEM((2, 2 * HID, LANES), bf16),
-        pltpu.VMEM((2, 4, 2 * HID, LANES), bf16)], 4)
+        pltpu.VMEM((2, 4, 2 * HID, LANES), bf16)], 4 * MIB)
 
 
 def run_all(feats, labels, w_in, w_out, mom_in, mom_out, step_size):
@@ -429,21 +463,22 @@
     hidden, chains, _ = w_in.shape
     f32, bf16 = jnp.float32, jnp.bfloat16
     state = struct((HID, LANES))
-    outs = [struct((SIDE, SIDE, SIDE, rows, LANES), bf16), struct((BLOCKS, rows // LANES, LANES, LANES), bf16), struct((BLOCKS, 8, LANES)), state, state]
-    *data, pos, vel = call(
-        collect_rows, 'collect', (feats, labels, w_in, w_out, mom_in, mom_out), outs,
-        [pltpu.VMEM((rows, num_feat), bf16), pltpu.VMEM((2, hidden, 8, num_feat), f32), DMA((3, 36)), DMA((3, 36)), DMA((3,))],
-        4, 0, [HBM, VMEM, HBM, VMEM, HBM, VMEM])
+    own, pos, vel = call(
+        prepare, 'prepare', (feats, labels, w_in, w_out, mom_in, mom_out), [struct((rows, LANES), bf16), state, state],
+        [pltpu.VMEM((rows, num_feat), bf16), pltpu.VMEM((2, hidden, 8, num_feat), f32), pltpu.VMEM((8, LANES), jnp.int32), pltpu.VMEM((2, hidden, chains), f32), DMA((6,))],
+        PREPARE_BYTES, None, [HBM] * 6)
+    outs = [struct((SIDE, SIDE, SIDE, rows, LANES), bf16), struct((BLOCKS, rows // LANES, LANES, LANES), bf16), struct((BLOCKS, 8, LANES))]
+    data = call(collect_rows, 'collect', (own,), outs, [DMA((3, 36)), DMA((3, 36)), DMA], 2 * MIB, 0)
     for k in range(LEAPS):
         part = grad_call(data, pos, False)
         rate = 0.5 * step_size if k == 0 else step_size
         pos, vel = call(functools.partial(leap, rate, step_size), 'leap', (part, pos, vel), [state, state],
-                        [pltpu.VMEM((HID, LANES), f32), DMA, DMA], 1, 1 if k == 0 else 2)
+                        [pltpu.VMEM((HID, LANES), f32), DMA, DMA], MIB, 1 if k == 0 else 2)
     part = grad_call(data, pos, True)
     every = call(functools.partial(finish, 0.5 * step_size, hidden), 'finish', (part, pos, vel), struct((2, SIDE, SIDE, SIDE, HID, LANES)),
-                 [pltpu.VMEM((HID, LANES), f32), DMA, DMA, DMA((3, 36)), DMA((3, 36)), DMA, DMA], 2, 3)
+                 [pltpu.VMEM((HID, LANES), f32), DMA, DMA, DMA((3, 36)), DMA((3, 36)), DMA((3, 4)), DMA((3, 4))], 2 * MIB, 3)
     ends = [struct(w_in.shape), struct(w_out.shape)] * 2 + [struct((1, chains))]
-    return call(spread_out, 'spread', (every.reshape(2, BLOCKS * HID, LANES),), ends, [], 8)
+    return call(spread_out, 'spread', (every.reshape(2, BLOCKS * HID, LANES),), ends, [], 8 * MIB)
 
 
 def solution(mesh):

time: 273 us -> 261 us (0.956)
  Pallas kernels: 265 us -> 258 us
  local copies, waits for them, and re-layouts: 5.98 us -> 1.69 us
    pallas_call x36 -> x37, Pallas kernels: 265 us -> 258 us  [call(): pl.pallas_call(kernel, out_shape=outs, in_specs=in_specs or [VMEM] * len(...]
    unnamed x12 -> x6, local copies, waits for them, and re-layouts: 5.98 us -> 1.69 us
where the time goes in v4:
time: 261 us
  Pallas kernels  258 us (99%)
    pallas_call x37, Pallas kernels, call(): pl.pallas_call(kernel, out_shape=outs, in_specs=in_specs or [VMEM] * len(...  258 us

profile of v4, /device:TPU:1, one launch (start us, length us, event | category | flops | bytes accessed | tf_op | source)
XLA Modules:
  0.0 261.0 jit_solution(12839774619304702713)
XLA Ops:
  0.6 2.0 prepare.1
  3.6 70.9 %collect.1 = (bf16[4,4,4,1024,128]{4,3,2,1,0:T(8,128)(2,1)S(1)}, bf16[64,8,128,128]{3,2,1,0:T(8,128)(2,1)S(1)}, f32[64,8,128]{2,1,0:T(8,128)S(1)}) custom-call(bf16[1024,128]{1,0:T(8,128)(2,1)S(1)} %copy-done), custom_call_target="tpu_custom_call" | custom-call | tf_op jit(solution)/shard_map/collect/pallas_call | solution.py:446
  75.3 7.9 %gradient.17.part_ref = f32[56,128]{1,0:T(8,128)S(1)} custom-call(bf16[4,4,4,1024,128]{4,3,2,1,0:T(8,128)(2,1)S(1)} %get-tuple-element.49.refs_0_, bf16[64,8,128,128]{3,2,1,0:T(8,128)(2,1)S(1)} %get-tuple-element.50.refs_1_, f32[64,8,128]{2,1,0:T(8,128)S(1)} %get-tuple-element.51.refs_2_, f32[56,128]{1,0:T(8,128)S(1)} %copy-done.1), custom_call_target="tpu_custom_call" | custom-call | tf_op jit(solution)/shard_map/gradient/pallas_call | solution.py:446
  83.2 4.8 %leap.16 = (f32[56,128]{1,0:T(8,128)S(1)}, f32[56,128]{1,0:T(8,128)S(1)}) custom-call(f32[56,128]{1,0:T(8,128)S(1)} %gradient.17.part_ref, f32[56,128]{1,0:T(8,128)S(1)} %copy-done.1, f32[56,128]{1,0:T(8,128)S(1)} %copy-done.2), custom_call_target="tpu_custom_call" | custom-call | tf_op jit(solution)/shard_map/leap/pallas_call | solution.py:446
  88.0 7.9 %gradient.18.part_ref = f32[56,128]{1,0:T(8,128)S(1)} custom-call(bf16[4,4,4,1024,128]{4,3,2,1,0:T(8,128)(2,1)S(1)} %get-tuple-element.49.refs_0_, bf16[64,8,128,128]{3,2,1,0:T(8,128)(2,1)S(1)} %get-tuple-element.50.refs_1_, f32[64,8,128]{2,1,0:T(8,128)S(1)} %get-tuple-element.51.refs_2_, f32[56,128]{1,0:T(8,128)S(1)} %get-tuple-element.54.refs_3_.pos_ref), custom_call_target="tpu_custom_call" | custom-call | tf_op jit(solution)/shard_map/gradient/pallas_call | solution.py:446
  95.9 1.3 leap.17
  97.1 7.9 %gradient.19.part_ref = f32[56,128]{1,0:T(8,128)S(1)} custom-call(bf16[4,4,4,1024,128]{4,3,2,1,0:T(8,128)(2,1)S(1)} %get-tuple-element.49.refs_0_, bf16[64,8,128,128]{3,2,1,0:T(8,128)(2,1)S(1)} %get-tuple-element.50.refs_1_, f32[64,8,128]{2,1,0:T(8,128)S(1)} %get-tuple-element.51.refs_2_, f32[56,128]{1,0:T(8,128)S(1)} %get-tuple-element.56.refs_3_.pos_ref), custom_call_target="tpu_custom_call" | custom-call | tf_op jit(solution)/shard_map/gradient/pallas_call | solution.py:446
  105.0 1.3 leap.18
  106.3 7.9 %gradient.20.part_ref = f32[56,128]{1,0:T(8,128)S(1)} custom-call(bf16[4,4,4,1024,128]{4,3,2,1,0:T(8,128)(2,1)S(1)} %get-tuple-element.49.refs_0_, bf16[64,8,128,128]{3,2,1,0:T(8,128)(2,1)S(1)} %get-tuple-element.50.refs_1_, f32[64,8,128]{2,1,0:T(8,128)S(1)} %get-tuple-element.51.refs_2_, f32[56,128]{1,0:T(8,128)S(1)} %get-tuple-element.58.refs_3_.pos_ref), custom_call_target="tpu_custom_call" | custom-call | tf_op jit(solution)/shard_map/gradient/pallas_call | solution.py:446
  114.2 1.3 leap.19
  115.5 7.9 %gradient.21.part_ref = f32[56,128]{1,0:T(8,128)S(1)} custom-call(bf16[4,4,4,1024,128]{4,3,2,1,0:T(8,128)(2,1)S(1)} %get-tuple-element.49.refs_0_, bf16[64,8,128,128]{3,2,1,0:T(8,128)(2,1)S(1)} %get-tuple-element.50.refs_1_, f32[64,8,128]{2,1,0:T(8,128)S(1)} %get-tuple-element.51.refs_2_, f32[56,128]{1,0:T(8,128)S(1)} %get-tuple-element.60.refs_3_.pos_ref), custom_call_target="tpu_custom_call" | custom-call | tf_op jit(solution)/shard_map/gradient/pallas_call | solution.py:446
  123.4 1.3 leap.20
  124.6 7.9 %gradient.22.part_ref = f32[56,128]{1,0:T(8,128)S(1)} custom-call(bf16[4,4,4,1024,128]{4,3,2,1,0:T(8,128)(2,1)S(1)} %get-tuple-element.49.refs_0_, bf16[64,8,128,128]{3,2,1,0:T(8,128)(2,1)S(1)} %get-tuple-element.50.refs_1_, f32[64,8,128]{2,1,0:T(8,128)S(1)} %get-tuple-element.51.refs_2_, f32[56,128]{1,0:T(8,128)S(1)} %get-tuple-element.62.refs_3_.pos_ref), custom_call_target="tpu_custom_call" | custom-call | tf_op jit(solution)/shard_map/gradient/pallas_call | solution.py:446
  132.5 1.3 leap.21
  133.8 7.9 %gradient.23.part_ref = f32[56,128]{1,0:T(8,128)S(1)} custom-call(bf16[4,4,4,1024,128]{4,3,2,1,0:T(8,128)(2,1)S(1)} %get-tuple-element.49.refs_0_, bf16[64,8,128,128]{3,2,1,0:T(8,128)(2,1)S(1)} %get-tuple-element.50.refs_1_, f32[64,8,128]{2,1,0:T(8,128)S(1)} %get-tuple-element.51.refs_2_, f32[56,128]{1,0:T(8,128)S(1)} %get-tuple-element.64.refs_3_.pos_ref), custom_call_target="tpu_custom_call" | custom-call | tf_op jit(solution)/shard_map/gradient/pallas_call | solution.py:446
  141.7 1.3 leap.22
  143.0 7.9 %gradient.24.part_ref = f32[56,128]{1,0:T(8,128)S(1)} custom-call(bf16[4,4,4,1024,128]{4,3,2,1,0:T(8,128)(2,1)S(1)} %get-tuple-element.49.refs_0_, bf16[64,8,128,128]{3,2,1,0:T(8,128)(2,1)S(1)} %get-tuple-element.50.refs_1_, f32[64,8,128]{2,1,0:T(8,128)S(1)} %get-tuple-element.51.refs_2_, f32[56,128]{1,0:T(8,128)S(1)} %get-tuple-element.66.refs_3_.pos_ref), custom_call_target="tpu_custom_call" | custom-call | tf_op jit(solution)/shard_map/gradient/pallas_call | solution.py:446
  152.1 7.9 %gradient.25.part_ref = f32[56,128]{1,0:T(8,128)S(1)} custom-call(bf16[4,4,4,1024,128]{4,3,2,1,0:T(8,128)(2,1)S(1)} %get-tuple-element.49.refs_0_, bf16[64,8,128,128]{3,2,1,0:T(8,128)(2,1)S(1)} %get-tuple-element.50.refs_1_, f32[64,8,128]{2,1,0:T(8,128)S(1)} %get-tuple-element.51.refs_2_, f32[56,128]{1,0:T(8,128)S(1)} %get-tuple-element.68.refs_3_.pos_ref), custom_call_target="tpu_custom_call" | custom-call | tf_op jit(solution)/shard_map/gradient/pallas_call | solution.py:446
  160.1 1.3 leap.24
  161.3 8.1 %gradient.26.part_ref = f32[56,128]{1,0:T(8,128)S(1)} custom-call(bf16[4,4,4,1024,128]{4,3,2,1,0:T(8,128)(2,1)S(1)} %get-tuple-element.49.refs_0_, bf16[64,8,128,128]{3,2,1,0:T(8,128)(2,1)S(1)} %get-tuple-element.50.refs_1_, f32[64,8,128]{2,1,0:T(8,128)S(1)} %get-tuple-element.51.refs_2_, f32[56,128]{1,0:T(8,128)S(1)} %get-tuple-element.70.refs_3_.pos_ref), custom_call_target="tpu_custom_call" | custom-call | tf_op jit(solution)/shard_map/gradient/pallas_call | solution.py:446
  170.7 7.9 %gradient.27.part_ref = f32[56,128]{1,0:T(8,128)S(1)} custom-call(bf16[4,4,4,1024,128]{4,3,2,1,0:T(8,128)(2,1)S(1)} %get-tuple-element.49.refs_0_, bf16[64,8,128,128]{3,2,1,0:T(8,128)(2,1)S(1)} %get-tuple-element.50.refs_1_, f32[64,8,128]{2,1,0:T(8,128)S(1)} %get-tuple-element.51.refs_2_, f32[56,128]{1,0:T(8,128)S(1)} %get-tuple-element.72.refs_3_.pos_ref), custom_call_target="tpu_custom_call" | custom-call | tf_op jit(solution)/shard_map/gradient/pallas_call | solution.py:446
  178.6 1.3 leap.26
  179.8 7.9 %gradient.28.part_ref = f32[56,128]{1,0:T(8,128)S(1)} custom-call(bf16[4,4,4,1024,128]{4,3,2,1,0:T(8,128)(2,1)S(1)} %get-tuple-element.49.refs_0_, bf16[64,8,128,128]{3,2,1,0:T(8,128)(2,1)S(1)} %get-tuple-element.50.refs_1_, f32[64,8,128]{2,1,0:T(8,128)S(1)} %get-tuple-element.51.refs_2_, f32[56,128]{1,0:T(8,128)S(1)} %get-tuple-element.74.refs_3_.pos_ref), custom_call_target="tpu_custom_call" | custom-call | tf_op jit(solution)/shard_map/gradient/pallas_call | solution.py:446
  189.0 7.9 %gradient.29.part_ref = f32[56,128]{1,0:T(8,128)S(1)} custom-call(bf16[4,4,4,1024,128]{4,3,2,1,0:T(8,128)(2,1)S(1)} %get-tuple-element.49.refs_0_, bf16[64,8,128,128]{3,2,1,0:T(8,128)(2,1)S(1)} %get-tuple-element.50.refs_1_, f32[64,8,128]{2,1,0:T(8,128)S(1)} %get-tuple-element.51.refs_2_, f32[56,128]{1,0:T(8,128)S(1)} %get-tuple-element.76.refs_3_.pos_ref), custom_call_target="tpu_custom_call" | custom-call | tf_op jit(solution)/shard_map/gradient/pallas_call | solution.py:446
  196.9 1.3 leap.28
  198.2 7.9 %gradient.30.part_ref = f32[56,128]{1,0:T(8,128)S(1)} custom-call(bf16[4,4,4,1024,128]{4,3,2,1,0:T(8,128)(2,1)S(1)} %get-tuple-element.49.refs_0_, bf16[64,8,128,128]{3,2,1,0:T(8,128)(2,1)S(1)} %get-tuple-element.50.refs_1_, f32[64,8,128]{2,1,0:T(8,128)S(1)} %get-tuple-element.51.refs_2_, f32[56,128]{1,0:T(8,128)S(1)} %get-tuple-element.78.refs_3_.pos_ref), custom_call_target="tpu_custom_call" | custom-call | tf_op jit(solution)/shard_map/gradient/pallas_call | solution.py:446
  207.3 7.9 %gradient.31.part_ref = f32[56,128]{1,0:T(8,128)S(1)} custom-call(bf16[4,4,4,1024,128]{4,3,2,1,0:T(8,128)(2,1)S(1)} %get-tuple-element.49.refs_0_, bf16[64,8,128,128]{3,2,1,0:T(8,128)(2,1)S(1)} %get-tuple-element.50.refs_1_, f32[64,8,128]{2,1,0:T(8,128)S(1)} %get-tuple-element.51.refs_2_, f32[56,128]{1,0:T(8,128)S(1)} %get-tuple-element.80.refs_3_.pos_ref), custom_call_target="tpu_custom_call" | custom-call | tf_op jit(solution)/shard_map/gradient/pallas_call | solution.py:446
  215.3 1.3 leap.30
  216.5 7.9 %gradient.32.part_ref = f32[56,128]{1,0:T(8,128)S(1)} custom-call(bf16[4,4,4,1024,128]{4,3,2,1,0:T(8,128)(2,1)S(1)} %get-tuple-element.49.refs_0_, bf16[64,8,128,128]{3,2,1,0:T(8,128)(2,1)S(1)} %get-tuple-element.50.refs_1_, f32[64,8,128]{2,1,0:T(8,128)S(1)} %get-tuple-element.51.refs_2_, f32[56,128]{1,0:T(8,128)S(1)} %get-tuple-element.82.refs_3_.pos_ref), custom_call_target="tpu_custom_call" | custom-call | tf_op jit(solution)/shard_map/gradient/pallas_call | solution.py:446
  225.7 9.5 %gradient.33.part_ref = f32[56,128]{1,0:T(8,128)S(1)} custom-call(bf16[4,4,4,1024,128]{4,3,2,1,0:T(8,128)(2,1)S(1)} %get-tuple-element.49.refs_0_, bf16[64,8,128,128]{3,2,1,0:T(8,128)(2,1)S(1)} %get-tuple-element.50.refs_1_, f32[64,8,128]{2,1,0:T(8,128)S(1)} %get-tuple-element.51.refs_2_, f32[56,128]{1,0:T(8,128)S(1)} %get-tuple-element.84.refs_3_.pos_ref), custom_call_target="tpu_custom_call" | custom-call | tf_op jit(solution)/shard_map/gradient/pallas_call | solution.py:446
  235.1 23.2 %finish.1 = f32[2,4,4,4,56,128]{5,4,3,2,1,0:T(8,128)S(1)} custom-call(f32[56,128]{1,0:T(8,128)S(1)} %gradient.33.part_ref, f32[56,128]{1,0:T(8,128)S(1)} %get-tuple-element.84.refs_3_.pos_ref, f32[56,128]{1,0:T(8,128)S(1)} %get-tuple-element.85.vel_ref), custom_call_target="tpu_custom_call" | custom-call | tf_op jit(solution)/shard_map/finish/pallas_call | solution.py:446
  258.4 2.7 %spread.1 = (f32[50,64,123]{2,1,0:T(8,128)}, f32[50,64]{1,0:T(8,128)}, f32[50,64,123]{2,1,0:T(8,128)}, f32[50,64]{1,0:T(8,128)}, f32[1,64]{1,0:T(1,128)}) custom-call(f32[2,3584,128]{2,1,0:T(8,128)S(1)} %bitcast.11), custom_call_target="tpu_custom_call" | custom-call | tf_op jit(solution)/shard_map/spread/pallas_call | solution.py:446
  (11 shorter events, 8.0 us)
Async XLA Ops:
  2.7 1.0 copy-start
  74.5 0.8 copy-start.1
  75.3 7.9 %copy-start.2 = (f32[56,128]{1,0:T(8,128)S(1)}, f32[56,128]{1,0:T(8,128)}, u32[]{:S(2)}) copy-start(f32[56,128]{1,0:T(8,128)} %get-tuple-element.53.vel_ref) | copy-start | bytes 86020

commit v5 on v4

--- a/solution.py
+++ b/solution.py
@@ -109,10 +109,10 @@
     for p in range(3):
         start_full(p, 2, at(p, None, 2, 0), B3 + 12)
     for q in range(4):
+        if q == 3 and near is not None:
+            near()
         for p in range(3):
             relay(p, 2, at(p, None, OFFS[q], -1), at(p, None, OFFS[q], 1), B3 + 4 * q)
-    if near is not None:
-        near()
     if share is not None:
         for p in range(3):
             for i in range(3):
@@ -165,6 +165,21 @@
     lane = lax.broadcasted_iota(jnp.int32, (HID, LANES), 1)
     sub = lax.broadcasted_iota(jnp.int32, (HID, LANES), 0)
     return lane, sub
+
+
+def set_weights(pos, wbd_ref, w2_ref):
+    lane, _ = grids()
+    w_in = jnp.where(lane < LAB, pos, 0.0)
+    nil = jnp.zeros_like(w_in)
+    wbd_ref[0] = jnp.concatenate([w_in, nil], axis=0).astype(jnp.bfloat16)
+    wbd_ref[1] = jnp.concatenate([nil, w_in], axis=0).astype(jnp.bfloat16)
+    w2_ref[...] = jnp.broadcast_to(pos[:, OUT:OUT + 1], (HID, LANES))
+
+
+def whole_gradient(whole, acc):
+    lane, _ = grids()
+    grad = whole[:HID, :LANES] + whole[HID:, LANES:]
+    return jnp.where(lane < LAB, grad, jnp.where(lane == OUT, jnp.sum(acc, axis=1, keepdims=True), 0.0))
 
 
 def prepare(feat_ref, lab_ref, w_ref, wo_ref, m_ref, mo_ref, own_ref, pos_ref, vel_ref, x_in, w_tmp, lab_tmp, o_tmp, sem):
@@ -197,13 +212,75 @@
         ref[:hidden, OUT:OUT + 1] = jnp.sum(jnp.where(chain_lane, o_tmp[n], 0.0), axis=1, keepdims=True)
 
 
-def collect_rows(own_ref, x_all, xt_all, y_all, x_send, x_recv, own_sem):
+def collect_rows(own_ref, pos_ref, x_all, xt_all, y_all, part_ref, w2_ref, wbd_ref, a_ref, zp_ref, b_ref, g_ref, acc_ref,
+                 x_send, x_recv, own_sem):
     core, chip, coords, partner, device_at = place()
     own = pltpu.make_async_copy(own_ref, x_all.at[coords[0], coords[1], coords[2]], own_sem)
     own.start()
     ready = greet(torus_neighbours(coords, device_at))
+    g_ref[...] = jnp.zeros_like(g_ref)
+    acc_ref[...] = jnp.zeros_like(acc_ref)
+    set_weights(pos_ref[...], wbd_ref, w2_ref)
     own.wait()
     ready()
+
+    def forward(b):
+        wbd = jnp.concatenate([wbd_ref[0], wbd_ref[1]], axis=1)
+        pres = []
+        for t in range(2):
+            tiles = [jnp.concatenate([xt_all[b, 4 * s + 2 * t], xt_all[b, 4 * s + 2 * t + 1]], axis=1) for s in range(2)]
+            pres.append(jnp.dot(wbd, jnp.concatenate(tiles, axis=0), preferred_element_type=jnp.float32))
+        return pres
+
+    def activate(pres, u):
+        w2 = w2_ref[...].reshape(HID // 8, 8, LANES)
+        for t in range(2):
+            act = jnp.tanh(pres[t])
+            for h in range(2):
+                j = 2 * t + h
+                a_ref[u, j] = act[:, h * LANES:(h + 1) * LANES]
+                for s in range(2):
+                    part = act[s * HID:(s + 1) * HID, h * LANES:(h + 1) * LANES].reshape(HID // 8, 8, LANES)
+                    k = 4 * s + j
+                    zp_ref[u, 8 * k:8 * k + 8, :] = jnp.sum(part * w2, axis=0)
+
+    def backward(b, u, acc):
+        z = zp_ref[u, pl.ds(0, 8, stride=8), :]
+        for k in range(1, 8):
+            z = z + zp_ref[u, pl.ds(k, 8, stride=8), :]
+        res = y_all[b] - 1.0 / (1.0 + jnp.exp(-z))
+        w2 = w2_ref[...]
+        for j in range(4):
+            parts = []
+            for s in range(2):
+                r = jnp.broadcast_to(res[4 * s + j:4 * s + j + 1, :], (HID, LANES))
+                act = a_ref[u, j, s * HID:(s + 1) * HID, :]
+                ra = r * act
+                acc = acc + ra
+                parts.append((r - ra * act) * w2)
+            b_ref[u, j] = jnp.concatenate(parts, axis=0).astype(jnp.bfloat16)
+        return acc
+
+    def weight_grad(where, u):
+        z, y, x = where
+        rows = x_all.at[z, y, x]
+        lhs = jnp.concatenate([b_ref[u, j] for j in range(4)], axis=1)
+        return jnp.dot(lhs, jnp.concatenate([rows[:512, :], rows[512:, :]], axis=1), preferred_element_type=jnp.float32)
+
+    def digest(wheres):
+        blocks = [(z * SIDE + y) * SIDE + x for z, y, x in wheres]
+        for where in wheres:
+            turn(where)
+        for u, b in enumerate(blocks):
+            activate(forward(b), u)
+        acc = acc_ref[...]
+        for u, b in enumerate(blocks):
+            acc = backward(b, u, acc)
+        acc_ref[...] = acc
+        part = weight_grad(wheres[0], 0)
+        for u in range(1, len(wheres)):
+            part = part + weight_grad(wheres[u], u)
+        g_ref[...] += part
 
     def turn(where):
         z, y, x = where
@@ -221,33 +298,25 @@
 
     def near():
         def body(i, carry):
-            turn(moved((three(i // 9), three((i // 3) % 3), three(i % 3))))
+            digest([moved((three(i), three(j // 3), three(j % 3))) for j in range(9)])
             return carry
-        lax.fori_loop(0, 27, body, 0)
+        lax.fori_loop(0, 3, body, 0)
 
     def middle():
         def body(i, carry):
-            u, v = three(i // 3), three(i % 3)
-            turn(moved((2, u, v)))
-            turn(moved((u, 2, v)))
-            turn(moved((u, v, 2)))
-            return carry
-        lax.fori_loop(0, 9, body, 0)
-
-    def far():
-        def body(i, carry):
             u = three(i)
-            turn(moved((2, 2, u)))
-            turn(moved((2, u, 2)))
-            turn(moved((u, 2, 2)))
+            digest([moved(o) for v in (three(0), three(1), three(2)) for o in ((2, u, v), (u, 2, v), (u, v, 2))])
             return carry
         lax.fori_loop(0, 3, body, 0)
-        turn(moved((2, 2, 2)))
+
+    def far():
+        digest([moved(o) for v in (three(0), three(1), three(2)) for o in ((2, 2, v), (2, v, 2), (v, 2, 2))] + [moved((2, 2, 2))])
 
     x_descs = torus_gather(x_all, ROW_PIECES, coords, device_at, x_send, x_recv, near, middle)
     far()
     for d in x_descs:
         d.wait_send()
+    part_ref[...] = whole_gradient(g_ref[...], acc_ref[...])
 
 
 def gradient(with_loss, *refs):
@@ -262,19 +331,19 @@
 
 def gradient_body(with_loss, pre_acc, grad_acc, x_all, xt_all, y_all, pos_ref, part_ref, z_all, w2_ref, wbd_ref, b_ref):
     lane, sub = grids()
-    def push_forward(b):
-        for q in range(2):
+    def push_forward(b, qs=(0, 1)):
+        for q in qs:
             tiles = [jnp.concatenate([xt_all[b, 4 * s + 2 * q], xt_all[b, 4 * s + 2 * q + 1]], axis=1) for s in range(2)]
             pltpu.matmul_push_rhs(jnp.concatenate(tiles, axis=0), staging_register=0, mxu_index=q)
 
-    def forward(u):
+    def forward(u, qs=(0, 1)):
         wbd = jnp.concatenate([wbd_ref[0], wbd_ref[1]], axis=1)
-        for q in range(2):
+        for q in qs:
             pltpu.matmul_acc_lhs(pre_acc[u][q], wbd, load_staged_rhs=0)
 
-    def rows_to_back(b, u, acc):
+    def rows_to_back(b, u, acc, qs=(0, 1)):
         w2 = w2_ref[...].reshape(HID // 8, 8, LANES)
-        for q in range(2):
+        for q in qs:
             act = jnp.tanh(pltpu.matmul_pop(pre_acc[u][q]))
             for h in range(2):
                 j = 2 * q + h
@@ -294,15 +363,15 @@
                 b_ref[u, j] = jnp.concatenate(parts, axis=0).astype(jnp.bfloat16)
         return acc
 
-    def push_grad(b):
+    def push_grad(b, qs=(0, 1)):
         z, y, x = block_index(b)
         rows = x_all.at[z, y, x]
-        for q in range(2):
+        for q in qs:
             tile = jnp.concatenate([rows[256 * q:256 * q + 256, :], rows[512 + 256 * q:768 + 256 * q, :]], axis=1)
             pltpu.matmul_push_rhs(tile, staging_register=1, mxu_index=q)
 
-    def weight_grad(u):
-        for q in range(2):
+    def weight_grad(u, qs=(0, 1)):
+        for q in qs:
             lhs = jnp.concatenate([b_ref[u, 2 * q], b_ref[u, 2 * q + 1]], axis=1)
             pltpu.matmul_acc_lhs(grad_acc[q], lhs, load_staged_rhs=1)
 
@@ -323,21 +392,25 @@
         for v in range(UNROLL):
             u = v % 2
             n = UNROLL * i + v
-            acc = rows_to_back(n, u, acc)
-            forward(u)
-            push_forward(jnp.minimum(n + 3, BLOCKS - 1))
-            weight_grad(1 - u)
-            push_grad(n)
+            acc = rows_to_back(n, u, acc, (0,))
+            forward(u, (0,))
+            push_forward(jnp.minimum(n + 3, BLOCKS - 1), (0,))
+            weight_grad(1 - u, (0,))
+            push_grad(n, (0,))
+            acc = rows_to_back(n, u, acc, (1,))
+            forward(u, (1,))
+            push_forward(jnp.minimum(n + 3, BLOCKS - 1), (1,))
+            weight_grad(1 - u, (1,))
+            push_grad(n, (1,))
         return acc
 
     acc = lax.fori_loop(0, BLOCKS // UNROLL, pair, jnp.zeros((HID // 8, 8, LANES), jnp.float32)).reshape(HID, LANES)
     weight_grad(1)
+    whole = pltpu.matmul_pop(grad_acc[0]) + pltpu.matmul_pop(grad_acc[1])
+    forward(0)
     for u in range(2):
-        if u == 0:
-            forward(u)
         for q in range(2):
             pltpu.matmul_pop(pre_acc[u][q])
-    whole = pltpu.matmul_pop(grad_acc[0]) + pltpu.matmul_pop(grad_acc[1])
     grad = whole[:HID, :LANES] + whole[HID:, LANES:]
     grad = jnp.where(lane < LAB, grad, jnp.where(lane == OUT, jnp.sum(acc, axis=1, keepdims=True), 0.0))
     if with_loss:
@@ -468,9 +541,13 @@
         [pltpu.VMEM((rows, num_feat), bf16), pltpu.VMEM((2, hidden, 8, num_feat), f32), pltpu.VMEM((8, LANES), jnp.int32), pltpu.VMEM((2, hidden, chains), f32), DMA((6,))],
         PREPARE_BYTES, None, [HBM] * 6)
     outs = [struct((SIDE, SIDE, SIDE, rows, LANES), bf16), struct((BLOCKS, rows // LANES, LANES, LANES), bf16), struct((BLOCKS, 8, LANES))]
-    data = call(collect_rows, 'collect', (own,), outs, [DMA((3, 36)), DMA((3, 36)), DMA], 2 * MIB, 0)
+    *data, part = call(collect_rows, 'collect', (own, pos), outs + [state], [
+        pltpu.VMEM((HID, LANES), f32), pltpu.VMEM((2, 2 * HID, LANES), bf16), pltpu.VMEM((10, 4, 2 * HID, LANES), f32),
+        pltpu.VMEM((10, 64, LANES), f32), pltpu.VMEM((10, 4, 2 * HID, LANES), bf16), pltpu.VMEM((2 * HID, 2 * LANES), f32),
+        pltpu.VMEM((HID, LANES), f32), DMA((3, 36)), DMA((3, 36)), DMA], 8 * MIB, 0)
     for k in range(LEAPS):
-        part = grad_call(data, pos, False)
+        if k > 0:
+            part = grad_call(data, pos, False)
         rate = 0.5 * step_size if k == 0 else step_size
         pos, vel = call(functools.partial(leap, rate, step_size), 'leap', (part, pos, vel), [state, state],
                         [pltpu.VMEM((HID, LANES), f32), DMA, DMA], MIB, 1 if k == 0 else 2)

time: 261 us -> 257 us (0.985)
  Pallas kernels: 258 us -> 253 us
    pallas_call x37 -> x36, Pallas kernels: 258 us -> 253 us  [call(): pl.pallas_call(kernel, out_shape=outs, in_specs=in_specs or [VMEM] * len(...]
where the time goes in v5:
time: 257 us; the launch traced here: 256 us
  Pallas kernels  253 us (98%)
    pallas_call x36, Pallas kernels, call(): pl.pallas_call(kernel, out_shape=outs, in_specs=in_specs or [VMEM] * len(...  253 us

profile of v5, /device:TPU:1, one launch (start us, length us, event | category | flops | bytes accessed | tf_op | source)
XLA Modules:
  0.0 256.4 jit_solution(10482889716652802491)
XLA Ops:
  0.6 2.0 prepare.1
  4.4 74.0 %collect.1 = (bf16[4,4,4,1024,128]{4,3,2,1,0:T(8,128)(2,1)S(1)}, bf16[64,8,128,128]{3,2,1,0:T(8,128)(2,1)S(1)}, f32[64,8,128]{2,1,0:T(8,128)S(1)}, f32[56,128]{1,0:T(8,128)S(1)}) custom-call(bf16[1024,128]{1,0:T(8,128)(2,1)S(1)} %copy-done, f32[56,128]{1,0:T(8,128)S(1)} %copy-done.1), custom_call_target="tpu_custom_call" | custom-call | tf_op jit(solution)/shard_map/collect/pallas_call | solution.py:519
  79.2 6.2 %leap.16 = (f32[56,128]{1,0:T(8,128)S(1)}, f32[56,128]{1,0:T(8,128)S(1)}) custom-call(f32[56,128]{1,0:T(8,128)S(1)} %get-tuple-element.54.part_ref, f32[56,128]{1,0:T(8,128)S(1)} %copy-done.1, f32[56,128]{1,0:T(8,128)S(1)} %copy-done.2), custom_call_target="tpu_custom_call" | custom-call | tf_op jit(solution)/shard_map/leap/pallas_call | solution.py:519
  85.4 7.8 %gradient.16.part_ref = f32[56,128]{1,0:T(8,128)S(1)} custom-call(bf16[4,4,4,1024,128]{4,3,2,1,0:T(8,128)(2,1)S(1)} %get-tuple-element.51.refs_0_, bf16[64,8,128,128]{3,2,1,0:T(8,128)(2,1)S(1)} %get-tuple-element.52.refs_1_, f32[64,8,128]{2,1,0:T(8,128)S(1)} %get-tuple-element.53.refs_2_, f32[56,128]{1,0:T(8,128)S(1)} %get-tuple-element.56.refs_3_.pos_ref), custom_call_target="tpu_custom_call" | custom-call | tf_op jit(solution)/shard_map/gradient/pallas_call | solution.py:519
  93.1 1.3 leap.17
  94.4 7.8 %gradient.17.part_ref = f32[56,128]{1,0:T(8,128)S(1)} custom-call(bf16[4,4,4,1024,128]{4,3,2,1,0:T(8,128)(2,1)S(1)} %get-tuple-element.51.refs_0_, bf16[64,8,128,128]{3,2,1,0:T(8,128)(2,1)S(1)} %get-tuple-element.52.refs_1_, f32[64,8,128]{2,1,0:T(8,128)S(1)} %get-tuple-element.53.refs_2_, f32[56,128]{1,0:T(8,128)S(1)} %get-tuple-element.58.refs_3_.pos_ref), custom_call_target="tpu_custom_call" | custom-call | tf_op jit(solution)/shard_map/gradient/pallas_call | solution.py:519
  102.2 1.2 leap.18
  103.5 7.8 %gradient.18.part_ref = f32[56,128]{1,0:T(8,128)S(1)} custom-call(bf16[4,4,4,1024,128]{4,3,2,1,0:T(8,128)(2,1)S(1)} %get-tuple-element.51.refs_0_, bf16[64,8,128,128]{3,2,1,0:T(8,128)(2,1)S(1)} %get-tuple-element.52.refs_1_, f32[64,8,128]{2,1,0:T(8,128)S(1)} %get-tuple-element.53.refs_2_, f32[56,128]{1,0:T(8,128)S(1)} %get-tuple-element.60.refs_3_.pos_ref), custom_call_target="tpu_custom_call" | custom-call | tf_op jit(solution)/shard_map/gradient/pallas_call | solution.py:519
  112.5 7.8 %gradient.19.part_ref = f32[56,128]{1,0:T(8,128)S(1)} custom-call(bf16[4,4,4,1024,128]{4,3,2,1,0:T(8,128)(2,1)S(1)} %get-tuple-element.51.refs_0_, bf16[64,8,128,128]{3,2,1,0:T(8,128)(2,1)S(1)} %get-tuple-element.52.refs_1_, f32[64,8,128]{2,1,0:T(8,128)S(1)} %get-tuple-element.53.refs_2_, f32[56,128]{1,0:T(8,128)S(1)} %get-tuple-element.62.refs_3_.pos_ref), custom_call_target="tpu_custom_call" | custom-call | tf_op jit(solution)/shard_map/gradient/pallas_call | solution.py:519
  120.3 1.2 leap.20
  121.5 7.8 %gradient.20.part_ref = f32[56,128]{1,0:T(8,128)S(1)} custom-call(bf16[4,4,4,1024,128]{4,3,2,1,0:T(8,128)(2,1)S(1)} %get-tuple-element.51.refs_0_, bf16[64,8,128,128]{3,2,1,0:T(8,128)(2,1)S(1)} %get-tuple-element.52.refs_1_, f32[64,8,128]{2,1,0:T(8,128)S(1)} %get-tuple-element.53.refs_2_, f32[56,128]{1,0:T(8,128)S(1)} %get-tuple-element.64.refs_3_.pos_ref), custom_call_target="tpu_custom_call" | custom-call | tf_op jit(solution)/shard_map/gradient/pallas_call | solution.py:519
  130.6 8.0 %gradient.21.part_ref = f32[56,128]{1,0:T(8,128)S(1)} custom-call(bf16[4,4,4,1024,128]{4,3,2,1,0:T(8,128)(2,1)S(1)} %get-tuple-element.51.refs_0_, bf16[64,8,128,128]{3,2,1,0:T(8,128)(2,1)S(1)} %get-tuple-element.52.refs_1_, f32[64,8,128]{2,1,0:T(8,128)S(1)} %get-tuple-element.53.refs_2_, f32[56,128]{1,0:T(8,128)S(1)} %get-tuple-element.66.refs_3_.pos_ref), custom_call_target="tpu_custom_call" | custom-call | tf_op jit(solution)/shard_map/gradient/pallas_call | solution.py:519
  138.6 1.2 leap.22
  139.8 7.8 %gradient.22.part_ref = f32[56,128]{1,0:T(8,128)S(1)} custom-call(bf16[4,4,4,1024,128]{4,3,2,1,0:T(8,128)(2,1)S(1)} %get-tuple-element.51.refs_0_, bf16[64,8,128,128]{3,2,1,0:T(8,128)(2,1)S(1)} %get-tuple-element.52.refs_1_, f32[64,8,128]{2,1,0:T(8,128)S(1)} %get-tuple-element.53.refs_2_, f32[56,128]{1,0:T(8,128)S(1)} %get-tuple-element.68.refs_3_.pos_ref), custom_call_target="tpu_custom_call" | custom-call | tf_op jit(solution)/shard_map/gradient/pallas_call | solution.py:519
  147.6 1.2 leap.23
  148.9 7.8 %gradient.23.part_ref = f32[56,128]{1,0:T(8,128)S(1)} custom-call(bf16[4,4,4,1024,128]{4,3,2,1,0:T(8,128)(2,1)S(1)} %get-tuple-element.51.refs_0_, bf16[64,8,128,128]{3,2,1,0:T(8,128)(2,1)S(1)} %get-tuple-element.52.refs_1_, f32[64,8,128]{2,1,0:T(8,128)S(1)} %get-tuple-element.53.refs_2_, f32[56,128]{1,0:T(8,128)S(1)} %get-tuple-element.70.refs_3_.pos_ref), custom_call_target="tpu_custom_call" | custom-call | tf_op jit(solution)/shard_map/gradient/pallas_call | solution.py:519
  156.6 1.2 leap.24
  157.9 7.8 %gradient.24.part_ref = f32[56,128]{1,0:T(8,128)S(1)} custom-call(bf16[4,4,4,1024,128]{4,3,2,1,0:T(8,128)(2,1)S(1)} %get-tuple-element.51.refs_0_, bf16[64,8,128,128]{3,2,1,0:T(8,128)(2,1)S(1)} %get-tuple-element.52.refs_1_, f32[64,8,128]{2,1,0:T(8,128)S(1)} %get-tuple-element.53.refs_2_, f32[56,128]{1,0:T(8,128)S(1)} %get-tuple-element.72.refs_3_.pos_ref), custom_call_target="tpu_custom_call" | custom-call | tf_op jit(solution)/shard_map/gradient/pallas_call | solution.py:519
  165.7 1.2 leap.25
  166.9 7.8 %gradient.25.part_ref = f32[56,128]{1,0:T(8,128)S(1)} custom-call(bf16[4,4,4,1024,128]{4,3,2,1,0:T(8,128)(2,1)S(1)} %get-tuple-element.51.refs_0_, bf16[64,8,128,128]{3,2,1,0:T(8,128)(2,1)S(1)} %get-tuple-element.52.refs_1_, f32[64,8,128]{2,1,0:T(8,128)S(1)} %get-tuple-element.53.refs_2_, f32[56,128]{1,0:T(8,128)S(1)} %get-tuple-element.74.refs_3_.pos_ref), custom_call_target="tpu_custom_call" | custom-call | tf_op jit(solution)/shard_map/gradient/pallas_call | solution.py:519
  174.7 1.2 leap.26
  176.0 7.8 %gradient.26.part_ref = f32[56,128]{1,0:T(8,128)S(1)} custom-call(bf16[4,4,4,1024,128]{4,3,2,1,0:T(8,128)(2,1)S(1)} %get-tuple-element.51.refs_0_, bf16[64,8,128,128]{3,2,1,0:T(8,128)(2,1)S(1)} %get-tuple-element.52.refs_1_, f32[64,8,128]{2,1,0:T(8,128)S(1)} %get-tuple-element.53.refs_2_, f32[56,128]{1,0:T(8,128)S(1)} %get-tuple-element.76.refs_3_.pos_ref), custom_call_target="tpu_custom_call" | custom-call | tf_op jit(solution)/shard_map/gradient/pallas_call | solution.py:519
  183.8 1.2 leap.27
  185.0 7.8 %gradient.27.part_ref = f32[56,128]{1,0:T(8,128)S(1)} custom-call(bf16[4,4,4,1024,128]{4,3,2,1,0:T(8,128)(2,1)S(1)} %get-tuple-element.51.refs_0_, bf16[64,8,128,128]{3,2,1,0:T(8,128)(2,1)S(1)} %get-tuple-element.52.refs_1_, f32[64,8,128]{2,1,0:T(8,128)S(1)} %get-tuple-element.53.refs_2_, f32[56,128]{1,0:T(8,128)S(1)} %get-tuple-element.78.refs_3_.pos_ref), custom_call_target="tpu_custom_call" | custom-call | tf_op jit(solution)/shard_map/gradient/pallas_call | solution.py:519
  192.8 1.2 leap.28
  194.1 7.8 %gradient.28.part_ref = f32[56,128]{1,0:T(8,128)S(1)} custom-call(bf16[4,4,4,1024,128]{4,3,2,1,0:T(8,128)(2,1)S(1)} %get-tuple-element.51.refs_0_, bf16[64,8,128,128]{3,2,1,0:T(8,128)(2,1)S(1)} %get-tuple-element.52.refs_1_, f32[64,8,128]{2,1,0:T(8,128)S(1)} %get-tuple-element.53.refs_2_, f32[56,128]{1,0:T(8,128)S(1)} %get-tuple-element.80.refs_3_.pos_ref), custom_call_target="tpu_custom_call" | custom-call | tf_op jit(solution)/shard_map/gradient/pallas_call | solution.py:519
  203.1 7.8 %gradient.29.part_ref = f32[56,128]{1,0:T(8,128)S(1)} custom-call(bf16[4,4,4,1024,128]{4,3,2,1,0:T(8,128)(2,1)S(1)} %get-tuple-element.51.refs_0_, bf16[64,8,128,128]{3,2,1,0:T(8,128)(2,1)S(1)} %get-tuple-element.52.refs_1_, f32[64,8,128]{2,1,0:T(8,128)S(1)} %get-tuple-element.53.refs_2_, f32[56,128]{1,0:T(8,128)S(1)} %get-tuple-element.82.refs_3_.pos_ref), custom_call_target="tpu_custom_call" | custom-call | tf_op jit(solution)/shard_map/gradient/pallas_call | solution.py:519
  210.9 1.2 leap.30
  212.2 7.8 %gradient.30.part_ref = f32[56,128]{1,0:T(8,128)S(1)} custom-call(bf16[4,4,4,1024,128]{4,3,2,1,0:T(8,128)(2,1)S(1)} %get-tuple-element.51.refs_0_, bf16[64,8,128,128]{3,2,1,0:T(8,128)(2,1)S(1)} %get-tuple-element.52.refs_1_, f32[64,8,128]{2,1,0:T(8,128)S(1)} %get-tuple-element.53.refs_2_, f32[56,128]{1,0:T(8,128)S(1)} %get-tuple-element.84.refs_3_.pos_ref), custom_call_target="tpu_custom_call" | custom-call | tf_op jit(solution)/shard_map/gradient/pallas_call | solution.py:519
  221.2 9.3 %gradient.31.part_ref = f32[56,128]{1,0:T(8,128)S(1)} custom-call(bf16[4,4,4,1024,128]{4,3,2,1,0:T(8,128)(2,1)S(1)} %get-tuple-element.51.refs_0_, bf16[64,8,128,128]{3,2,1,0:T(8,128)(2,1)S(1)} %get-tuple-element.52.refs_1_, f32[64,8,128]{2,1,0:T(8,128)S(1)} %get-tuple-element.53.refs_2_, f32[56,128]{1,0:T(8,128)S(1)} %get-tuple-element.86.refs_3_.pos_ref), custom_call_target="tpu_custom_call" | custom-call | tf_op jit(solution)/shard_map/gradient/pallas_call | solution.py:519
  230.5 23.2 %finish.1 = f32[2,4,4,4,56,128]{5,4,3,2,1,0:T(8,128)S(1)} custom-call(f32[56,128]{1,0:T(8,128)S(1)} %gradient.31.part_ref, f32[56,128]{1,0:T(8,128)S(1)} %get-tuple-element.86.refs_3_.pos_ref, f32[56,128]{1,0:T(8,128)S(1)} %get-tuple-element.87.vel_ref), custom_call_target="tpu_custom_call" | custom-call | tf_op jit(solution)/shard_map/finish/pallas_call | solution.py:519
  253.7 2.7 %spread.1 = (f32[50,64,123]{2,1,0:T(8,128)}, f32[50,64]{1,0:T(8,128)}, f32[50,64,123]{2,1,0:T(8,128)}, f32[50,64]{1,0:T(8,128)}, f32[1,64]{1,0:T(1,128)}) custom-call(f32[2,3584,128]{2,1,0:T(8,128)S(1)} %bitcast.11), custom_call_target="tpu_custom_call" | custom-call | tf_op jit(solution)/shard_map/spread/pallas_call | solution.py:519
  (10 shorter events, 7.4 us)
Async XLA Ops:
  2.7 1.0 copy-start
  3.6 0.7 copy-start.1
  78.4 0.8 copy-start.2

commit v6 on v5

--- a/solution.py
+++ b/solution.py
@@ -118,10 +118,10 @@
             for i in range(3):
                 share(p, i, at(p, None, None, OFFS[i]))
     for q in range(4):
-        if q == 3 and middle is not None:
-            middle()
         for p in range(3):
             finish(p, 2, at(p, None, OFFS[q], 2), B3 + 4 * q)
+        if q < 3 and middle is not None:
+            middle(q)
     if share is not None:
         for p in range(3):
             share(p, 3, at(p, None, None, 2))
@@ -302,12 +302,9 @@
             return carry
         lax.fori_loop(0, 3, body, 0)
 
-    def middle():
-        def body(i, carry):
-            u = three(i)
-            digest([moved(o) for v in (three(0), three(1), three(2)) for o in ((2, u, v), (u, 2, v), (u, v, 2))])
-            return carry
-        lax.fori_loop(0, 3, body, 0)
+    def middle(q):
+        u = (0, 3, 1)[q]
+        digest([moved(o) for v in (0, 3, 1) for o in ((v, u, 2), (2, v, u), (u, 2, v))])
 
     def far():
         digest([moved(o) for v in (three(0), three(1), three(2)) for o in ((2, 2, v), (2, v, 2), (v, 2, 2))] + [moved((2, 2, 2))])

time: 257 us -> 253 us (0.984)
  Pallas kernels: 253 us -> 249 us
    pallas_call x36, Pallas kernels: 253 us -> 249 us  [call(): pl.pallas_call(kernel, out_shape=outs, in_specs=in_specs or [VMEM] * len(...]
where the time goes in v6:
time: 253 us
  Pallas kernels  249 us (98%)
    pallas_call x36, Pallas kernels, call(): pl.pallas_call(kernel, out_shape=outs, in_specs=in_specs or [VMEM] * len(...  249 us

profile of v6, /device:TPU:1, one launch (start us, length us, event | category | flops | bytes accessed | tf_op | source)
XLA Modules:
  0.0 252.8 jit_solution(8765923458283976100)
XLA Ops:
  0.6 2.0 prepare.1
  4.4 72.2 %collect.1 = (bf16[4,4,4,1024,128]{4,3,2,1,0:T(8,128)(2,1)S(1)}, bf16[64,8,128,128]{3,2,1,0:T(8,128)(2,1)S(1)}, f32[64,8,128]{2,1,0:T(8,128)S(1)}, f32[56,128]{1,0:T(8,128)S(1)}) custom-call(bf16[1024,128]{1,0:T(8,128)(2,1)S(1)} %copy-done, f32[56,128]{1,0:T(8,128)S(1)} %copy-done.1), custom_call_target="tpu_custom_call" | custom-call | tf_op jit(solution)/shard_map/collect/pallas_call | solution.py:516
  77.4 4.2 %leap.16 = (f32[56,128]{1,0:T(8,128)S(1)}, f32[56,128]{1,0:T(8,128)S(1)}) custom-call(f32[56,128]{1,0:T(8,128)S(1)} %get-tuple-element.54.part_ref, f32[56,128]{1,0:T(8,128)S(1)} %copy-done.1, f32[56,128]{1,0:T(8,128)S(1)} %copy-done.2), custom_call_target="tpu_custom_call" | custom-call | tf_op jit(solution)/shard_map/leap/pallas_call | solution.py:516
  81.6 7.8 %gradient.16.part_ref = f32[56,128]{1,0:T(8,128)S(1)} custom-call(bf16[4,4,4,1024,128]{4,3,2,1,0:T(8,128)(2,1)S(1)} %get-tuple-element.51.refs_0_, bf16[64,8,128,128]{3,2,1,0:T(8,128)(2,1)S(1)} %get-tuple-element.52.refs_1_, f32[64,8,128]{2,1,0:T(8,128)S(1)} %get-tuple-element.53.refs_2_, f32[56,128]{1,0:T(8,128)S(1)} %get-tuple-element.56.refs_3_.pos_ref), custom_call_target="tpu_custom_call" | custom-call | tf_op jit(solution)/shard_map/gradient/pallas_call | solution.py:516
  89.4 1.2 leap.17
  90.6 7.8 %gradient.17.part_ref = f32[56,128]{1,0:T(8,128)S(1)} custom-call(bf16[4,4,4,1024,128]{4,3,2,1,0:T(8,128)(2,1)S(1)} %get-tuple-element.51.refs_0_, bf16[64,8,128,128]{3,2,1,0:T(8,128)(2,1)S(1)} %get-tuple-element.52.refs_1_, f32[64,8,128]{2,1,0:T(8,128)S(1)} %get-tuple-element.53.refs_2_, f32[56,128]{1,0:T(8,128)S(1)} %get-tuple-element.58.refs_3_.pos_ref), custom_call_target="tpu_custom_call" | custom-call | tf_op jit(solution)/shard_map/gradient/pallas_call | solution.py:516
  98.4 1.3 leap.18
  99.7 8.0 %gradient.18.part_ref = f32[56,128]{1,0:T(8,128)S(1)} custom-call(bf16[4,4,4,1024,128]{4,3,2,1,0:T(8,128)(2,1)S(1)} %get-tuple-element.51.refs_0_, bf16[64,8,128,128]{3,2,1,0:T(8,128)(2,1)S(1)} %get-tuple-element.52.refs_1_, f32[64,8,128]{2,1,0:T(8,128)S(1)} %get-tuple-element.53.refs_2_, f32[56,128]{1,0:T(8,128)S(1)} %get-tuple-element.60.refs_3_.pos_ref), custom_call_target="tpu_custom_call" | custom-call | tf_op jit(solution)/shard_map/gradient/pallas_call | solution.py:516
  107.7 1.2 leap.19
  108.9 7.8 %gradient.19.part_ref = f32[56,128]{1,0:T(8,128)S(1)} custom-call(bf16[4,4,4,1024,128]{4,3,2,1,0:T(8,128)(2,1)S(1)} %get-tuple-element.51.refs_0_, bf16[64,8,128,128]{3,2,1,0:T(8,128)(2,1)S(1)} %get-tuple-element.52.refs_1_, f32[64,8,128]{2,1,0:T(8,128)S(1)} %get-tuple-element.53.refs_2_, f32[56,128]{1,0:T(8,128)S(1)} %get-tuple-element.62.refs_3_.pos_ref), custom_call_target="tpu_custom_call" | custom-call | tf_op jit(solution)/shard_map/gradient/pallas_call | solution.py:516
  116.7 1.2 leap.20
  118.0 7.8 %gradient.20.part_ref = f32[56,128]{1,0:T(8,128)S(1)} custom-call(bf16[4,4,4,1024,128]{4,3,2,1,0:T(8,128)(2,1)S(1)} %get-tuple-element.51.refs_0_, bf16[64,8,128,128]{3,2,1,0:T(8,128)(2,1)S(1)} %get-tuple-element.52.refs_1_, f32[64,8,128]{2,1,0:T(8,128)S(1)} %get-tuple-element.53.refs_2_, f32[56,128]{1,0:T(8,128)S(1)} %get-tuple-element.64.refs_3_.pos_ref), custom_call_target="tpu_custom_call" | custom-call | tf_op jit(solution)/shard_map/gradient/pallas_call | solution.py:516
  125.7 1.2 leap.21
  127.0 7.8 %gradient.21.part_ref = f32[56,128]{1,0:T(8,128)S(1)} custom-call(bf16[4,4,4,1024,128]{4,3,2,1,0:T(8,128)(2,1)S(1)} %get-tuple-element.51.refs_0_, bf16[64,8,128,128]{3,2,1,0:T(8,128)(2,1)S(1)} %get-tuple-element.52.refs_1_, f32[64,8,128]{2,1,0:T(8,128)S(1)} %get-tuple-element.53.refs_2_, f32[56,128]{1,0:T(8,128)S(1)} %get-tuple-element.66.refs_3_.pos_ref), custom_call_target="tpu_custom_call" | custom-call | tf_op jit(solution)/shard_map/gradient/pallas_call | solution.py:516
  134.8 1.2 leap.22
  136.0 7.8 %gradient.22.part_ref = f32[56,128]{1,0:T(8,128)S(1)} custom-call(bf16[4,4,4,1024,128]{4,3,2,1,0:T(8,128)(2,1)S(1)} %get-tuple-element.51.refs_0_, bf16[64,8,128,128]{3,2,1,0:T(8,128)(2,1)S(1)} %get-tuple-element.52.refs_1_, f32[64,8,128]{2,1,0:T(8,128)S(1)} %get-tuple-element.53.refs_2_, f32[56,128]{1,0:T(8,128)S(1)} %get-tuple-element.68.refs_3_.pos_ref), custom_call_target="tpu_custom_call" | custom-call | tf_op jit(solution)/shard_map/gradient/pallas_call | solution.py:516
  143.8 1.2 leap.23
  145.1 7.8 %gradient.23.part_ref = f32[56,128]{1,0:T(8,128)S(1)} custom-call(bf16[4,4,4,1024,128]{4,3,2,1,0:T(8,128)(2,1)S(1)} %get-tuple-element.51.refs_0_, bf16[64,8,128,128]{3,2,1,0:T(8,128)(2,1)S(1)} %get-tuple-element.52.refs_1_, f32[64,8,128]{2,1,0:T(8,128)S(1)} %get-tuple-element.53.refs_2_, f32[56,128]{1,0:T(8,128)S(1)} %get-tuple-element.70.refs_3_.pos_ref), custom_call_target="tpu_custom_call" | custom-call | tf_op jit(solution)/shard_map/gradient/pallas_call | solution.py:516
  152.9 1.2 leap.24
  154.1 7.8 %gradient.24.part_ref = f32[56,128]{1,0:T(8,128)S(1)} custom-call(bf16[4,4,4,1024,128]{4,3,2,1,0:T(8,128)(2,1)S(1)} %get-tuple-element.51.refs_0_, bf16[64,8,128,128]{3,2,1,0:T(8,128)(2,1)S(1)} %get-tuple-element.52.refs_1_, f32[64,8,128]{2,1,0:T(8,128)S(1)} %get-tuple-element.53.refs_2_, f32[56,128]{1,0:T(8,128)S(1)} %get-tuple-element.72.refs_3_.pos_ref), custom_call_target="tpu_custom_call" | custom-call | tf_op jit(solution)/shard_map/gradient/pallas_call | solution.py:516
  163.2 7.8 %gradient.25.part_ref = f32[56,128]{1,0:T(8,128)S(1)} custom-call(bf16[4,4,4,1024,128]{4,3,2,1,0:T(8,128)(2,1)S(1)} %get-tuple-element.51.refs_0_, bf16[64,8,128,128]{3,2,1,0:T(8,128)(2,1)S(1)} %get-tuple-element.52.refs_1_, f32[64,8,128]{2,1,0:T(8,128)S(1)} %get-tuple-element.53.refs_2_, f32[56,128]{1,0:T(8,128)S(1)} %get-tuple-element.74.refs_3_.pos_ref), custom_call_target="tpu_custom_call" | custom-call | tf_op jit(solution)/shard_map/gradient/pallas_call | solution.py:516
  171.0 1.2 leap.26
  172.2 7.8 %gradient.26.part_ref = f32[56,128]{1,0:T(8,128)S(1)} custom-call(bf16[4,4,4,1024,128]{4,3,2,1,0:T(8,128)(2,1)S(1)} %get-tuple-element.51.refs_0_, bf16[64,8,128,128]{3,2,1,0:T(8,128)(2,1)S(1)} %get-tuple-element.52.refs_1_, f32[64,8,128]{2,1,0:T(8,128)S(1)} %get-tuple-element.53.refs_2_, f32[56,128]{1,0:T(8,128)S(1)} %get-tuple-element.76.refs_3_.pos_ref), custom_call_target="tpu_custom_call" | custom-call | tf_op jit(solution)/shard_map/gradient/pallas_call | solution.py:516
  181.3 7.8 %gradient.27.part_ref = f32[56,128]{1,0:T(8,128)S(1)} custom-call(bf16[4,4,4,1024,128]{4,3,2,1,0:T(8,128)(2,1)S(1)} %get-tuple-element.51.refs_0_, bf16[64,8,128,128]{3,2,1,0:T(8,128)(2,1)S(1)} %get-tuple-element.52.refs_1_, f32[64,8,128]{2,1,0:T(8,128)S(1)} %get-tuple-element.53.refs_2_, f32[56,128]{1,0:T(8,128)S(1)} %get-tuple-element.78.refs_3_.pos_ref), custom_call_target="tpu_custom_call" | custom-call | tf_op jit(solution)/shard_map/gradient/pallas_call | solution.py:516
  189.1 1.2 leap.28
  190.3 7.8 %gradient.28.part_ref = f32[56,128]{1,0:T(8,128)S(1)} custom-call(bf16[4,4,4,1024,128]{4,3,2,1,0:T(8,128)(2,1)S(1)} %get-tuple-element.51.refs_0_, bf16[64,8,128,128]{3,2,1,0:T(8,128)(2,1)S(1)} %get-tuple-element.52.refs_1_, f32[64,8,128]{2,1,0:T(8,128)S(1)} %get-tuple-element.53.refs_2_, f32[56,128]{1,0:T(8,128)S(1)} %get-tuple-element.80.refs_3_.pos_ref), custom_call_target="tpu_custom_call" | custom-call | tf_op jit(solution)/shard_map/gradient/pallas_call | solution.py:516
  199.4 8.0 %gradient.29.part_ref = f32[56,128]{1,0:T(8,128)S(1)} custom-call(bf16[4,4,4,1024,128]{4,3,2,1,0:T(8,128)(2,1)S(1)} %get-tuple-element.51.refs_0_, bf16[64,8,128,128]{3,2,1,0:T(8,128)(2,1)S(1)} %get-tuple-element.52.refs_1_, f32[64,8,128]{2,1,0:T(8,128)S(1)} %get-tuple-element.53.refs_2_, f32[56,128]{1,0:T(8,128)S(1)} %get-tuple-element.82.refs_3_.pos_ref), custom_call_target="tpu_custom_call" | custom-call | tf_op jit(solution)/shard_map/gradient/pallas_call | solution.py:516
  207.4 1.2 leap.30
  208.6 7.8 %gradient.30.part_ref = f32[56,128]{1,0:T(8,128)S(1)} custom-call(bf16[4,4,4,1024,128]{4,3,2,1,0:T(8,128)(2,1)S(1)} %get-tuple-element.51.refs_0_, bf16[64,8,128,128]{3,2,1,0:T(8,128)(2,1)S(1)} %get-tuple-element.52.refs_1_, f32[64,8,128]{2,1,0:T(8,128)S(1)} %get-tuple-element.53.refs_2_, f32[56,128]{1,0:T(8,128)S(1)} %get-tuple-element.84.refs_3_.pos_ref), custom_call_target="tpu_custom_call" | custom-call | tf_op jit(solution)/shard_map/gradient/pallas_call | solution.py:516
  217.7 9.3 %gradient.31.part_ref = f32[56,128]{1,0:T(8,128)S(1)} custom-call(bf16[4,4,4,1024,128]{4,3,2,1,0:T(8,128)(2,1)S(1)} %get-tuple-element.51.refs_0_, bf16[64,8,128,128]{3,2,1,0:T(8,128)(2,1)S(1)} %get-tuple-element.52.refs_1_, f32[64,8,128]{2,1,0:T(8,128)S(1)} %get-tuple-element.53.refs_2_, f32[56,128]{1,0:T(8,128)S(1)} %get-tuple-element.86.refs_3_.pos_ref), custom_call_target="tpu_custom_call" | custom-call | tf_op jit(solution)/shard_map/gradient/pallas_call | solution.py:516
  226.9 23.2 %finish.1 = f32[2,4,4,4,56,128]{5,4,3,2,1,0:T(8,128)S(1)} custom-call(f32[56,128]{1,0:T(8,128)S(1)} %gradient.31.part_ref, f32[56,128]{1,0:T(8,128)S(1)} %get-tuple-element.86.refs_3_.pos_ref, f32[56,128]{1,0:T(8,128)S(1)} %get-tuple-element.87.vel_ref), custom_call_target="tpu_custom_call" | custom-call | tf_op jit(solution)/shard_map/finish/pallas_call | solution.py:516
  250.1 2.7 %spread.1 = (f32[50,64,123]{2,1,0:T(8,128)}, f32[50,64]{1,0:T(8,128)}, f32[50,64,123]{2,1,0:T(8,128)}, f32[50,64]{1,0:T(8,128)}, f32[1,64]{1,0:T(1,128)}) custom-call(f32[2,3584,128]{2,1,0:T(8,128)S(1)} %bitcast.11), custom_call_target="tpu_custom_call" | custom-call | tf_op jit(solution)/shard_map/spread/pallas_call | solution.py:516
  (10 shorter events, 7.4 us)
Async XLA Ops:
  2.7 1.0 copy-start
  3.6 0.7 copy-start.1
  76.6 0.8 copy-start.2
